TPU v7x, 1024 devices: a whole 8x8x8 slice. The times are simulated.
1024 devices in a mesh: gx: 16 (over z, core), gy: 8 (over x), gz: 8 (over y).
Axes of the slice: x: 8, y: 8, z: 8, core: 2. Of those that a mesh axis runs over, the one named last changes fastest.
Arguments:
- right_side: bfloat16 [64, 1024, 1024], P('gz', 'gx', 'gy'), may hold values from -6 to 6
- phase_mask: int32 [64, 1024, 1024], P('gz', 'gx', 'gy'), may hold values from 0 to 1, as said below
Outputs:
- pressure: float32 [64, 1024, 1024], P('gz', 'gx', 'gy')
- scaled_residual: float32 [64, 1024, 1024], P('gz', 'gx', 'gy')
Inputs may be any that keep to these rules, and one draw needn't show every extreme that they name: `phase_mask`: 0 for a gas cell, 1 for a liquid cell.
All inputs are finite; a program needn't handle non-finite values.
Results may differ from a plain program's by a relative error of at most 0.0004.
Values may be sent and summed in bfloat16 or wider, within the bound.
A program may use at most 32 MiB of HBM per device.

v0:
```python
import functools

import jax
import jax.numpy as jnp
from jax import lax
from jax.sharding import Mesh
from jax.sharding import PartitionSpec as P

ITERS = 3
GX_GY_GZ = ("gx_0", "gx_1", "gy", "gz")
GX = ("gx_0", "gx_1")


density_ratio = 1000.0
mass_shift = 0.05


def extended(array, sides, width):
    edges = {}
    for axis, dim in sides:
        devices, length = (lax.axis_size(axis), array.shape[dim])
        up = [(i, (i + 1) % devices) for i in range(devices)]
        last = lax.slice_in_dim(array, length - width, length, axis=dim)
        first = lax.slice_in_dim(array, 0, width, axis=dim)
        edges[dim] = (
            lax.ppermute(last, axis, up),
            lax.ppermute(first, axis, [(b, a) for a, b in up]),
        )
    done = []
    for _, dim in sides:
        low, high = edges[dim]
        around = [(width, width) if d in done else (0, 0) for d in range(array.ndim)]
        array = jnp.concatenate([jnp.pad(low, around), array, jnp.pad(high, around)], axis=dim)
        done.append(dim)
    return array


def over_axes(array, axes):
    return functools.reduce(lax.psum, axes, array)


def neighbour(padded, axis, start):
    window = [slice(1, -1), slice(1, -1), slice(1, -1)]
    length = padded.shape[axis] - 2
    window[axis] = slice(start, start + length)
    return padded[tuple(window)]


def centre(padded):
    return padded[1:-1, 1:-1, 1:-1]


def apply_padded(field, padded, weights):
    total = mass_shift * field
    for weight, axis, start in weights:
        total = total + weight * (field - neighbour(padded, axis, start))
    return total


def operate(field, weights):
    padded = extended(field, ((GX, 1), ("gy", 2), ("gz", 0)), 1)
    return apply_padded(field, padded, weights)


def products(first, second, third, fourth):
    return (
        over_axes(jnp.sum(first * second), GX_GY_GZ),
        over_axes(jnp.sum(third * fourth), GX_GY_GZ),
    )


def build_weights(density_padded):
    density = centre(density_padded)
    weights = []
    diagonal = jnp.full(density.shape, mass_shift, jnp.float32)
    for axis in range(3):
        for start in (0, 2):
            weight = 2.0 / (density + neighbour(density_padded, axis, start))
            weights.append((weight, axis, start))
            diagonal = diagonal + weight
    return (weights, diagonal)


def on_device(right_side, phase_mask):
    mask_padded = extended(phase_mask, ((GX, 1), ("gy", 2), ("gz", 0)), 1)
    density_padded = 1.0 + (density_ratio - 1.0) * mask_padded.astype(jnp.float32)
    weights, diagonal = build_weights(density_padded)
    source = diagonal * right_side.astype(jnp.float32)
    smoothed = source / diagonal
    first_padded = extended(
        smoothed.astype(jnp.bfloat16), ((GX, 1), ("gy", 2), ("gz", 0)), 1
    ).astype(smoothed.dtype)
    applied = apply_padded(smoothed, first_padded, weights)
    pressure = jnp.zeros_like(source)
    residual = source
    direction = smoothed
    direction_image = applied
    scaled_update = smoothed
    twice_update = applied
    energy_old = jnp.float32(1.0)
    step_old = jnp.float32(1.0)
    for iteration in range(ITERS):
        energy, curvature = products(residual, smoothed, applied, smoothed)
        final_turn = iteration + 1 == ITERS
        if not final_turn:
            scaled_applied = applied / diagonal
            applied_twice = operate(scaled_applied, weights)
        if iteration == 0:
            step_size = energy / curvature
            direction = smoothed
            direction_image = applied
            scaled_update = scaled_applied
            twice_update = applied_twice
        else:
            factor = energy / energy_old
            step_size = energy / (curvature - factor * energy / step_old)
            direction = smoothed + factor * direction
            direction_image = applied + factor * direction_image
            if not final_turn:
                scaled_update = scaled_applied + factor * scaled_update
                twice_update = applied_twice + factor * twice_update
        pressure = pressure + step_size * direction
        residual = residual - step_size * direction_image
        if not final_turn:
            smoothed = smoothed - step_size * scaled_update
            applied = applied - step_size * twice_update
        energy_old = energy
        step_old = step_size
    return (pressure, residual / diagonal)


def solution(mesh):
    finer = Mesh(
        mesh.devices.reshape(8, 2, mesh.shape["gy"], mesh.shape["gz"]), ("gx_0", "gx_1", "gy", "gz")
    )
    placed = (P("gz", GX, "gy"), P("gz", GX, "gy"))
    return jax.shard_map(
        on_device,
        mesh=finer,
        in_specs=placed,
        out_specs=(P("gz", GX, "gy"), P("gz", GX, "gy")),
        check_vma=False,
    )
```

profile of v0, /device:TPU:2, one launch (start us, length us, event | category | flops | bytes accessed | tf_op | source)
XLA Modules:
  0.0 277.0 jit_solution(18368439770526600359)
XLA Ops:
  1.4 3.6 %collective-permute-start = (s32[1,64,128]{2,1,0:T(8,128)S(1)}, s32[1,64,128]{2,1,0:T(8,128)S(1)}, u32[]{:S(2)}, u32[]{:S(2)}) collective-permute-start(s32[1,64,128]{2,1,0:T(8,128)S(1)} %get-tuple-element.62), channel_id=1, source_target_pairs={{0,1},{1,2},{2,3},{3,4},{4,5},{5,6},{6,7},{7,0},{8,9},{9,10},{10,1... | collective-permute-start | bytes 98312 | tf_op jit(solution)/shard_map/ppermute | solution.py:26
  5.0 4.6 %collective-permute-start.5 = (s32[1,64,128]{2,1,0:T(8,128)S(1)}, s32[1,64,128]{2,1,0:T(8,128)S(1)}, u32[]{:S(2)}, u32[]{:S(2)}) collective-permute-start(s32[1,64,128]{2,1,0:T(8,128)S(1)} %get-tuple-element.63), channel_id=1, source_target_pairs={{1,0},{2,1},{3,2},{4,3},{5,4},{6,5},{7,6},{0,7},{9,8},{10,9},{11,1... | collective-permute-start | bytes 98312 | tf_op jit(solution)/shard_map/ppermute | solution.py:27
  10.8 3.4 %collective-permute-start.1 = (s32[8,64,1]{2,1,0:T(8,128)S(1)}, s32[8,64,1]{2,1,0:T(8,128)S(1)}, u32[]{:S(2)}, u32[]{:S(2)}) collective-permute-start(s32[8,64,1]{2,1,0:T(8,128)S(1)} %get-tuple-element.64), channel_id=1, source_target_pairs={{0,8},{8,16},{16,24},{24,32},{32,40},{40,48},{48,56},{56,0},{1,9},... | collective-permute-start | bytes 6152 | tf_op jit(solution)/shard_map/ppermute | solution.py:26
  14.3 14.3 %collective-permute-start.3 = (s32[8,1,128]{2,1,0:T(1,128)S(1)}, s32[8,1,128]{2,1,0:T(1,128)S(1)}, u32[]{:S(2)}, u32[]{:S(2)}) collective-permute-start(s32[8,1,128]{2,1,0:T(1,128)S(1)} %get-tuple-element.61), channel_id=1, source_target_pairs={{64,0},{128,64},{192,128},{256,192},{320,256},{384,320},{448,384},... | collective-permute-start | bytes 12296 | tf_op jit(solution)/shard_map/ppermute | solution.py:27
  29.2 5.3 %collective-permute-start.4 = (s32[8,64,1]{2,1,0:T(8,128)S(1)}, s32[8,64,1]{2,1,0:T(8,128)S(1)}, u32[]{:S(2)}, u32[]{:S(2)}) collective-permute-start(s32[8,64,1]{2,1,0:T(8,128)S(1)} %get-tuple-element.65), channel_id=1, source_target_pairs={{8,0},{16,8},{24,16},{32,24},{40,32},{48,40},{56,48},{0,56},{9,1},... | collective-permute-start | bytes 6152 | tf_op jit(solution)/shard_map/ppermute | solution.py:27
  34.4 3.9 %collective-permute-done.4 = s32[8,64,1]{2,1,0:T(8,128)S(1)} collective-permute-done((s32[8,64,1]{2,1,0:T(8,128)S(1)}, s32[8,64,1]{2,1,0:T(8,128)S(1)}, u32[]{:S(2)}, u32[]{:S(2)}) %collective-permute-start.4) | collective-permute-done | bytes 2080 | tf_op jit(solution)/shard_map/ppermute | solution.py:27
  41.3 5.1 %collective-permute-start.11 = (bf16[1,64,128]{2,1,0:T(8,128)(2,1)S(1)}, bf16[1,64,128]{2,1,0:T(8,128)(2,1)S(1)}, u32[]{:S(2)}, u32[]{:S(2)}) collective-permute-start(bf16[1,64,128]{2,1,0:T(8,128)(2,1)S(1)} %get-tuple-element.69), channel_id=1, source_target_pairs={{1,0},{2,1},{3,2},{4,3},{5,4},{6,5},{7,6},{0,7},{9,8},{10,9},{11,1... | collective-permute-start | bytes 49160 | tf_op jit(solution)/shard_map/ppermute | solution.py:27
  49.2 3.8 %collective-permute-start.9 = (bf16[8,1,128]{2,1,0:T(2,128)(2,1)S(1)}, bf16[8,1,128]{2,1,0:T(2,128)(2,1)S(1)}, u32[]{:S(2)}, u32[]{:S(2)}) collective-permute-start(bf16[8,1,128]{2,1,0:T(2,128)(2,1)S(1)} %get-tuple-element.67), channel_id=1, source_target_pairs={{64,0},{128,64},{192,128},{256,192},{320,256},{384,320},{448,384},... | collective-permute-start | bytes 6152 | tf_op jit(solution)/shard_map/ppermute | solution.py:27
  53.8 5.1 %collective-permute-start.10 = (bf16[8,64,1]{2,1,0:T(8,128)(2,1)S(1)}, bf16[8,64,1]{2,1,0:T(8,128)(2,1)S(1)}, u32[]{:S(2)}, u32[]{:S(2)}) collective-permute-start(bf16[8,64,1]{2,1,0:T(8,128)(2,1)S(1)} %get-tuple-element.71), channel_id=1, source_target_pairs={{8,0},{16,8},{24,16},{32,24},{40,32},{48,40},{56,48},{0,56},{9,1},... | collective-permute-start | bytes 3080 | tf_op jit(solution)/shard_map/ppermute | solution.py:27
  65.4 5.1 %collective-permute-start.17 = (f32[1,64,128]{2,1,0:T(8,128)S(1)}, f32[1,64,128]{2,1,0:T(8,128)S(1)}, u32[]{:S(2)}, u32[]{:S(2)}) collective-permute-start(f32[1,64,128]{2,1,0:T(8,128)S(1)} %get-tuple-element.55), channel_id=1, source_target_pairs={{1,0},{2,1},{3,2},{4,3},{5,4},{6,5},{7,6},{0,7},{9,8},{10,9},{11,1... | collective-permute-start | bytes 98312 | tf_op jit(solution)/shard_map/ppermute | solution.py:27
  70.5 3.9 %collective-permute-start.13 = (f32[8,64,1]{2,1,0:T(8,128)S(1)}, f32[8,64,1]{2,1,0:T(8,128)S(1)}, u32[]{:S(2)}, u32[]{:S(2)}) collective-permute-start(f32[8,64,1]{2,1,0:T(8,128)S(1)} %get-tuple-element.56), channel_id=1, source_target_pairs={{0,8},{8,16},{16,24},{24,32},{32,40},{40,48},{48,56},{56,0},{1,9},... | collective-permute-start | bytes 6152 | tf_op jit(solution)/shard_map/ppermute | solution.py:26
  78.8 5.1 %collective-permute-start.16 = (f32[8,64,1]{2,1,0:T(8,128)S(1)}, f32[8,64,1]{2,1,0:T(8,128)S(1)}, u32[]{:S(2)}, u32[]{:S(2)}) collective-permute-start(f32[8,64,1]{2,1,0:T(8,128)S(1)} %get-tuple-element.57), channel_id=1, source_target_pairs={{8,0},{16,8},{24,16},{32,24},{40,32},{48,40},{56,48},{0,56},{9,1},... | collective-permute-start | bytes 6152 | tf_op jit(solution)/shard_map/ppermute | solution.py:27
  83.9 20.6 %all-reduce.24 = (f32[]{:T(128)}, f32[]{:T(128)}) all-reduce(f32[]{:T(128)} %get-tuple-element.5, f32[]{:T(128)} %get-tuple-element.4), channel_id=1, replica_groups=mesh['gx_0'=8,'gx_1'=2,'gy'=8,'gz'=8] {'gx_0'}, use_global_device_ids=true, to_apply=%region_1.2 | all-reduce | flops 2 | bytes 16 | tf_op jit(solution)/shard_map/psum | solution.py:39
  107.6 16.4 %all-reduce.21 = (f32[]{:T(128)}, f32[]{:T(128)}) all-reduce(f32[]{:T(128)} %get-tuple-element.30, f32[]{:T(128)} %get-tuple-element.31), channel_id=1, replica_groups=mesh['gx_0'=8,'gx_1'=2,'gy'=8,'gz'=8] {'gy'}, use_global_device_ids=true, to_apply=%region_3.4 | all-reduce | flops 2 | bytes 16 | tf_op jit(solution)/shard_map/psum | solution.py:39
  124.0 14.9 %all-reduce.18 = (f32[]{:T(128)}, f32[]{:T(128)}) all-reduce(f32[]{:T(128)} %get-tuple-element.18, f32[]{:T(128)} %get-tuple-element.19), channel_id=1, replica_groups=mesh['gx_0'=8,'gx_1'=2,'gy'=8,'gz'=8] {'gz'}, use_global_device_ids=true, to_apply=%region_4.5 | all-reduce | flops 2 | bytes 16 | tf_op jit(solution)/shard_map/psum | solution.py:39
  148.3 3.9 %collective-permute-start.18 = (f32[1,64,128]{2,1,0:T(8,128)}, f32[1,64,128]{2,1,0:T(8,128)}, u32[]{:S(2)}, u32[]{:S(2)}) collective-permute-start(f32[1,64,128]{2,1,0:T(8,128)} %get-tuple-element.48), channel_id=1, source_target_pairs={{0,1},{1,2},{2,3},{3,4},{4,5},{5,6},{6,7},{7,0},{8,9},{9,10},{10,1... | collective-permute-start | bytes 98312 | tf_op jit(solution)/shard_map/ppermute | solution.py:26
  152.2 3.1 %collective-permute-start.23 = (f32[1,64,128]{2,1,0:T(8,128)}, f32[1,64,128]{2,1,0:T(8,128)}, u32[]{:S(2)}, u32[]{:S(2)}) collective-permute-start(f32[1,64,128]{2,1,0:T(8,128)} %get-tuple-element.49), channel_id=1, source_target_pairs={{1,0},{2,1},{3,2},{4,3},{5,4},{6,5},{7,6},{0,7},{9,8},{10,9},{11,1... | collective-permute-start | bytes 98312 | tf_op jit(solution)/shard_map/ppermute | solution.py:27
  159.3 14.8 %all-reduce.23 = (f32[]{:T(128)}, f32[]{:T(128)}) all-reduce(f32[]{:T(128)} %get-tuple-element.3, f32[]{:T(128)} %get-tuple-element.2), channel_id=1, replica_groups=mesh['gx_0'=8,'gx_1'=2,'gy'=8,'gz'=8] {'gx_0'}, use_global_device_ids=true, to_apply=%region_11.12 | all-reduce | flops 2 | bytes 16 | tf_op jit(solution)/shard_map/psum | solution.py:39
  174.1 3.2 %all-reduce.26 = (f32[]{:T(128)}, f32[]{:T(128)}) all-reduce(f32[]{:T(128)} %get-tuple-element.22, f32[]{:T(128)} %get-tuple-element.23), channel_id=1, replica_groups=mesh['gx_0'=8,'gx_1'=2,'gy'=8,'gz'=8] {'gx_1'}, use_global_device_ids=true, to_apply=%region_12.13 | all-reduce | flops 2 | bytes 16 | tf_op jit(solution)/shard_map/psum | solution.py:39
  177.3 18.0 %all-reduce.20 = (f32[]{:T(128)}, f32[]{:T(128)}) all-reduce(f32[]{:T(128)} %get-tuple-element.28, f32[]{:T(128)} %get-tuple-element.29), channel_id=1, replica_groups=mesh['gx_0'=8,'gx_1'=2,'gy'=8,'gz'=8] {'gy'}, use_global_device_ids=true, to_apply=%region_13.14 | all-reduce | flops 2 | bytes 16 | tf_op jit(solution)/shard_map/psum | solution.py:39
  195.3 16.8 %all-reduce.17 = (f32[]{:T(128)}, f32[]{:T(128)}) all-reduce(f32[]{:T(128)} %get-tuple-element.16, f32[]{:T(128)} %get-tuple-element.17), channel_id=1, replica_groups=mesh['gx_0'=8,'gx_1'=2,'gy'=8,'gz'=8] {'gz'}, use_global_device_ids=true, to_apply=%region_14.15 | all-reduce | flops 2 | bytes 16 | tf_op jit(solution)/shard_map/psum | solution.py:39
  220.3 16.8 %all-reduce.22 = (f32[]{:T(128)}, f32[]{:T(128)}) all-reduce(f32[]{:T(128)} %get-tuple-element.7, f32[]{:T(128)} %get-tuple-element.6), channel_id=1, replica_groups=mesh['gx_0'=8,'gx_1'=2,'gy'=8,'gz'=8] {'gx_0'}, use_global_device_ids=true, to_apply=%region_21.22 | all-reduce | flops 2 | bytes 16 | tf_op jit(solution)/shard_map/psum | solution.py:39
  240.3 14.9 %all-reduce.19 = (f32[]{:T(128)}, f32[]{:T(128)}) all-reduce(f32[]{:T(128)} %get-tuple-element.26, f32[]{:T(128)} %get-tuple-element.27), channel_id=1, replica_groups=mesh['gx_0'=8,'gx_1'=2,'gy'=8,'gz'=8] {'gy'}, use_global_device_ids=true, to_apply=%region_23.24 | all-reduce | flops 2 | bytes 16 | tf_op jit(solution)/shard_map/psum | solution.py:39
  255.2 16.1 %all-reduce.16 = (f32[]{:T(128)}, f32[]{:T(128)}) all-reduce(f32[]{:T(128)} %get-tuple-element.14, f32[]{:T(128)} %get-tuple-element.15), channel_id=1, replica_groups=mesh['gx_0'=8,'gx_1'=2,'gy'=8,'gz'=8] {'gz'}, use_global_device_ids=true, to_apply=%region_24.25 | all-reduce | flops 2 | bytes 16 | tf_op jit(solution)/shard_map/psum | solution.py:39
  (65 shorter events, 43.7 us)
Async XLA Ops:
  1.4 36.9 %collective-permute-start = (s32[1,64,128]{2,1,0:T(8,128)S(1)}, s32[1,64,128]{2,1,0:T(8,128)S(1)}, u32[]{:S(2)}, u32[]{:S(2)}) collective-permute-start(s32[1,64,128]{2,1,0:T(8,128)S(1)} %get-tuple-element.62), channel_id=1, source_target_pairs={{0,1},{1,2},{2,3},{3,4},{4,5},{5,6},{6,7},{7,0},{8,9},{9,10},{10,1... | collective-permute-start | bytes 98312 | tf_op jit(solution)/shard_map/ppermute | solution.py:26
  5.0 33.3 %collective-permute-start.5 = (s32[1,64,128]{2,1,0:T(8,128)S(1)}, s32[1,64,128]{2,1,0:T(8,128)S(1)}, u32[]{:S(2)}, u32[]{:S(2)}) collective-permute-start(s32[1,64,128]{2,1,0:T(8,128)S(1)} %get-tuple-element.63), channel_id=1, source_target_pairs={{1,0},{2,1},{3,2},{4,3},{5,4},{6,5},{7,6},{0,7},{9,8},{10,9},{11,1... | collective-permute-start | bytes 98312 | tf_op jit(solution)/shard_map/ppermute | solution.py:27
  10.8 18.4 %collective-permute-start.1 = (s32[8,64,1]{2,1,0:T(8,128)S(1)}, s32[8,64,1]{2,1,0:T(8,128)S(1)}, u32[]{:S(2)}, u32[]{:S(2)}) collective-permute-start(s32[8,64,1]{2,1,0:T(8,128)S(1)} %get-tuple-element.64), channel_id=1, source_target_pairs={{0,8},{8,16},{16,24},{24,32},{32,40},{40,48},{48,56},{56,0},{1,9},... | collective-permute-start | bytes 6152 | tf_op jit(solution)/shard_map/ppermute | solution.py:26
  14.3 24.1 %collective-permute-start.2 = (s32[8,1,128]{2,1,0:T(1,128)S(1)}, s32[8,1,128]{2,1,0:T(1,128)S(1)}, u32[]{:S(2)}, u32[]{:S(2)}) collective-permute-start(s32[8,1,128]{2,1,0:T(1,128)S(1)} %get-tuple-element.60), channel_id=1, source_target_pairs={{0,64},{64,128},{128,192},{192,256},{256,320},{320,384},{384,448},... | collective-permute-start | bytes 12296 | tf_op jit(solution)/shard_map/ppermute | solution.py:26
  14.3 24.0 %collective-permute-start.3 = (s32[8,1,128]{2,1,0:T(1,128)S(1)}, s32[8,1,128]{2,1,0:T(1,128)S(1)}, u32[]{:S(2)}, u32[]{:S(2)}) collective-permute-start(s32[8,1,128]{2,1,0:T(1,128)S(1)} %get-tuple-element.61), channel_id=1, source_target_pairs={{64,0},{128,64},{192,128},{256,192},{320,256},{384,320},{448,384},... | collective-permute-start | bytes 12296 | tf_op jit(solution)/shard_map/ppermute | solution.py:27
  29.2 9.1 %collective-permute-start.4 = (s32[8,64,1]{2,1,0:T(8,128)S(1)}, s32[8,64,1]{2,1,0:T(8,128)S(1)}, u32[]{:S(2)}, u32[]{:S(2)}) collective-permute-start(s32[8,64,1]{2,1,0:T(8,128)S(1)} %get-tuple-element.65), channel_id=1, source_target_pairs={{8,0},{16,8},{24,16},{32,24},{40,32},{48,40},{56,48},{0,56},{9,1},... | collective-permute-start | bytes 6152 | tf_op jit(solution)/shard_map/ppermute | solution.py:27
  39.4 22.4 %collective-permute-start.6 = (bf16[1,64,128]{2,1,0:T(8,128)(2,1)S(1)}, bf16[1,64,128]{2,1,0:T(8,128)(2,1)S(1)}, u32[]{:S(2)}, u32[]{:S(2)}) collective-permute-start(bf16[1,64,128]{2,1,0:T(8,128)(2,1)S(1)} %get-tuple-element.68), channel_id=1, source_target_pairs={{0,1},{1,2},{2,3},{3,4},{4,5},{5,6},{6,7},{7,0},{8,9},{9,10},{10,1... | collective-permute-start | bytes 49160 | tf_op jit(solution)/shard_map/ppermute | solution.py:26
  41.3 20.5 %collective-permute-start.11 = (bf16[1,64,128]{2,1,0:T(8,128)(2,1)S(1)}, bf16[1,64,128]{2,1,0:T(8,128)(2,1)S(1)}, u32[]{:S(2)}, u32[]{:S(2)}) collective-permute-start(bf16[1,64,128]{2,1,0:T(8,128)(2,1)S(1)} %get-tuple-element.69), channel_id=1, source_target_pairs={{1,0},{2,1},{3,2},{4,3},{5,4},{6,5},{7,6},{0,7},{9,8},{10,9},{11,1... | collective-permute-start | bytes 49160 | tf_op jit(solution)/shard_map/ppermute | solution.py:27
  46.4 7.3 %collective-permute-start.7 = (bf16[8,64,1]{2,1,0:T(8,128)(2,1)S(1)}, bf16[8,64,1]{2,1,0:T(8,128)(2,1)S(1)}, u32[]{:S(2)}, u32[]{:S(2)}) collective-permute-start(bf16[8,64,1]{2,1,0:T(8,128)(2,1)S(1)} %get-tuple-element.70), channel_id=1, source_target_pairs={{0,8},{8,16},{16,24},{24,32},{32,40},{40,48},{48,56},{56,0},{1,9},... | collective-permute-start | bytes 3080 | tf_op jit(solution)/shard_map/ppermute | solution.py:26
  49.2 12.6 %collective-permute-start.8 = (bf16[8,1,128]{2,1,0:T(2,128)(2,1)S(1)}, bf16[8,1,128]{2,1,0:T(2,128)(2,1)S(1)}, u32[]{:S(2)}, u32[]{:S(2)}) collective-permute-start(bf16[8,1,128]{2,1,0:T(2,128)(2,1)S(1)} %get-tuple-element.66), channel_id=1, source_target_pairs={{0,64},{64,128},{128,192},{192,256},{256,320},{320,384},{384,448},... | collective-permute-start | bytes 6152 | tf_op jit(solution)/shard_map/ppermute | solution.py:26
  49.2 12.6 %collective-permute-start.9 = (bf16[8,1,128]{2,1,0:T(2,128)(2,1)S(1)}, bf16[8,1,128]{2,1,0:T(2,128)(2,1)S(1)}, u32[]{:S(2)}, u32[]{:S(2)}) collective-permute-start(bf16[8,1,128]{2,1,0:T(2,128)(2,1)S(1)} %get-tuple-element.67), channel_id=1, source_target_pairs={{64,0},{128,64},{192,128},{256,192},{320,256},{384,320},{448,384},... | collective-permute-start | bytes 6152 | tf_op jit(solution)/shard_map/ppermute | solution.py:27
  53.8 8.0 %collective-permute-start.10 = (bf16[8,64,1]{2,1,0:T(8,128)(2,1)S(1)}, bf16[8,64,1]{2,1,0:T(8,128)(2,1)S(1)}, u32[]{:S(2)}, u32[]{:S(2)}) collective-permute-start(bf16[8,64,1]{2,1,0:T(8,128)(2,1)S(1)} %get-tuple-element.71), channel_id=1, source_target_pairs={{8,0},{16,8},{24,16},{32,24},{40,32},{48,40},{56,48},{0,56},{9,1},... | collective-permute-start | bytes 3080 | tf_op jit(solution)/shard_map/ppermute | solution.py:27
  63.4 76.9 %collective-permute-start.12 = (f32[1,64,128]{2,1,0:T(8,128)S(1)}, f32[1,64,128]{2,1,0:T(8,128)S(1)}, u32[]{:S(2)}, u32[]{:S(2)}) collective-permute-start(f32[1,64,128]{2,1,0:T(8,128)S(1)} %get-tuple-element.54), channel_id=1, source_target_pairs={{0,1},{1,2},{2,3},{3,4},{4,5},{5,6},{6,7},{7,0},{8,9},{9,10},{10,1... | collective-permute-start | bytes 98312 | tf_op jit(solution)/shard_map/ppermute | solution.py:26
  65.4 75.0 %collective-permute-start.17 = (f32[1,64,128]{2,1,0:T(8,128)S(1)}, f32[1,64,128]{2,1,0:T(8,128)S(1)}, u32[]{:S(2)}, u32[]{:S(2)}) collective-permute-start(f32[1,64,128]{2,1,0:T(8,128)S(1)} %get-tuple-element.55), channel_id=1, source_target_pairs={{1,0},{2,1},{3,2},{4,3},{5,4},{6,5},{7,6},{0,7},{9,8},{10,9},{11,1... | collective-permute-start | bytes 98312 | tf_op jit(solution)/shard_map/ppermute | solution.py:27
  70.5 8.3 %collective-permute-start.13 = (f32[8,64,1]{2,1,0:T(8,128)S(1)}, f32[8,64,1]{2,1,0:T(8,128)S(1)}, u32[]{:S(2)}, u32[]{:S(2)}) collective-permute-start(f32[8,64,1]{2,1,0:T(8,128)S(1)} %get-tuple-element.56), channel_id=1, source_target_pairs={{0,8},{8,16},{16,24},{24,32},{32,40},{40,48},{48,56},{56,0},{1,9},... | collective-permute-start | bytes 6152 | tf_op jit(solution)/shard_map/ppermute | solution.py:26
  74.4 65.9 %collective-permute-start.14 = (f32[8,1,128]{2,1,0:T(1,128)S(1)}, f32[8,1,128]{2,1,0:T(1,128)S(1)}, u32[]{:S(2)}, u32[]{:S(2)}) collective-permute-start(f32[8,1,128]{2,1,0:T(1,128)S(1)} %get-tuple-element.58), channel_id=1, source_target_pairs={{0,64},{64,128},{128,192},{192,256},{256,320},{320,384},{384,448},... | collective-permute-start | bytes 12296 | tf_op jit(solution)/shard_map/ppermute | solution.py:26
  74.5 65.9 %collective-permute-start.15 = (f32[8,1,128]{2,1,0:T(1,128)S(1)}, f32[8,1,128]{2,1,0:T(1,128)S(1)}, u32[]{:S(2)}, u32[]{:S(2)}) collective-permute-start(f32[8,1,128]{2,1,0:T(1,128)S(1)} %get-tuple-element.59), channel_id=1, source_target_pairs={{64,0},{128,64},{192,128},{256,192},{320,256},{384,320},{448,384},... | collective-permute-start | bytes 12296 | tf_op jit(solution)/shard_map/ppermute | solution.py:27
  78.8 61.5 %collective-permute-start.16 = (f32[8,64,1]{2,1,0:T(8,128)S(1)}, f32[8,64,1]{2,1,0:T(8,128)S(1)}, u32[]{:S(2)}, u32[]{:S(2)}) collective-permute-start(f32[8,64,1]{2,1,0:T(8,128)S(1)} %get-tuple-element.57), channel_id=1, source_target_pairs={{8,0},{16,8},{24,16},{32,24},{40,32},{48,40},{56,48},{0,56},{9,1},... | collective-permute-start | bytes 6152 | tf_op jit(solution)/shard_map/ppermute | solution.py:27
  142.3 13.1 %collective-permute-start.19 = (f32[8,64,1]{2,1,0:T(8,128)S(1)}, f32[8,64,1]{2,1,0:T(8,128)S(1)}, u32[]{:S(2)}, u32[]{:S(2)}) collective-permute-start(f32[8,64,1]{2,1,0:T(8,128)S(1)} %get-tuple-element.50), channel_id=1, source_target_pairs={{0,8},{8,16},{16,24},{24,32},{32,40},{40,48},{48,56},{56,0},{1,9},... | collective-permute-start | bytes 6152 | tf_op jit(solution)/shard_map/ppermute | solution.py:26
  145.3 72.3 %collective-permute-start.20 = (f32[8,1,128]{2,1,0:T(1,128)S(1)}, f32[8,1,128]{2,1,0:T(1,128)S(1)}, u32[]{:S(2)}, u32[]{:S(2)}) collective-permute-start(f32[8,1,128]{2,1,0:T(1,128)S(1)} %get-tuple-element.52), channel_id=1, source_target_pairs={{0,64},{64,128},{128,192},{192,256},{256,320},{320,384},{384,448},... | collective-permute-start | bytes 12296 | tf_op jit(solution)/shard_map/ppermute | solution.py:26
  145.3 72.2 %collective-permute-start.21 = (f32[8,1,128]{2,1,0:T(1,128)S(1)}, f32[8,1,128]{2,1,0:T(1,128)S(1)}, u32[]{:S(2)}, u32[]{:S(2)}) collective-permute-start(f32[8,1,128]{2,1,0:T(1,128)S(1)} %get-tuple-element.53), channel_id=1, source_target_pairs={{64,0},{128,64},{192,128},{256,192},{320,256},{384,320},{448,384},... | collective-permute-start | bytes 12296 | tf_op jit(solution)/shard_map/ppermute | solution.py:27
  148.3 69.3 %collective-permute-start.18 = (f32[1,64,128]{2,1,0:T(8,128)}, f32[1,64,128]{2,1,0:T(8,128)}, u32[]{:S(2)}, u32[]{:S(2)}) collective-permute-start(f32[1,64,128]{2,1,0:T(8,128)} %get-tuple-element.48), channel_id=1, source_target_pairs={{0,1},{1,2},{2,3},{3,4},{4,5},{5,6},{6,7},{7,0},{8,9},{9,10},{10,1... | collective-permute-start | bytes 98312 | tf_op jit(solution)/shard_map/ppermute | solution.py:26
  152.2 65.4 %collective-permute-start.23 = (f32[1,64,128]{2,1,0:T(8,128)}, f32[1,64,128]{2,1,0:T(8,128)}, u32[]{:S(2)}, u32[]{:S(2)}) collective-permute-start(f32[1,64,128]{2,1,0:T(8,128)} %get-tuple-element.49), channel_id=1, source_target_pairs={{1,0},{2,1},{3,2},{4,3},{5,4},{6,5},{7,6},{0,7},{9,8},{10,9},{11,1... | collective-permute-start | bytes 98312 | tf_op jit(solution)/shard_map/ppermute | solution.py:27
  155.3 61.2 %collective-permute-start.22 = (f32[8,64,1]{2,1,0:T(8,128)}, f32[8,64,1]{2,1,0:T(8,128)}, u32[]{:S(2)}, u32[]{:S(2)}) collective-permute-start(f32[8,64,1]{2,1,0:T(8,128)} %get-tuple-element.51), channel_id=1, source_target_pairs={{8,0},{16,8},{24,16},{32,24},{40,32},{48,40},{56,48},{0,56},{9,1},... | collective-permute-start | bytes 6152 | tf_op jit(solution)/shard_map/ppermute | solution.py:27
  (2 other events, 18.8 us)
where the time goes:
time: 279 us; the launch traced here: 277 us
  blocking collectives  159 us (57%)
  starting transfers between devices  85.1 us (31%)
  between operations  10.6 us (4%)
  waiting for transfers between devices  9.59 us (3%)
  other arithmetic  8.36 us (3%)
  local copies, waits for them, and re-layouts  4.73 us (2%)
    psum x12, blocking collectives, over_axes(): return functools.reduce(lax.psum, axes, array)  159 us
    ppermute x12, starting transfers between devices, extended(): lax.ppermute(first, axis, [(b, a) for a, b in up])  60.6 us
    ppermute x12, starting transfers between devices, extended(): lax.ppermute(last, axis, up)  24.5 us
    ppermute x12, waiting for transfers between devices, extended(): lax.ppermute(first, axis, [(b, a) for a, b in up])  6.77 us
  transfers between devices with their start and end apart: 24, of which 5 were waited for; matrix products, arithmetic and copies ran while one was open for 1% of the time, Pallas kernels for 0%

commit v1 on v0

v1 whole, which is shorter than its diff:
```python
import functools

import jax
import jax.numpy as jnp
from jax import lax
from jax.experimental import pallas as pl
from jax.experimental.pallas import tpu as pltpu
from jax.sharding import PartitionSpec as P

MESH = pl.DeviceIdType.MESH
F32 = jnp.float32
BF16 = jnp.bfloat16

mass_shift = 0.05
GAS = 1.0
MIXED = 2.0 / 1001.0
LIQUID = 0.001

NZ, NX, NY = 8, 64, 128
PAD = 16
ROWS = NX + 2 * PAD
LO, HI = PAD - 8, PAD + NX + 8
R = slice(LO, HI)
OWN = slice(8, 8 + NX)


def halo_offsets():
    out = []
    for dz in (-1, 0, 1):
        for dx in (-1, 0, 1):
            for dy in (-1, 0, 1):
                if (dz, dx, dy) != (0, 0, 0):
                    out.append((dz, dx, dy))
    return out


def kernel(sizes, rhs_hbm, mask_hbm, p_ref, r_ref, maskv, edge, pack, left, right,
           v0, mk, wx, wy, wz, di, u1, u2, u3, mine, got, in_sem, hs, hr, rs, rr):
    gz, gx, gy = sizes
    iz, ix, iy = (lax.axis_index(a) for a in ("gz", "gx", "gy"))

    def device(dz, dx, dy):
        return {
            "gz": lax.rem(iz + (dz % gz), gz),
            "gx": lax.rem(ix + (dx % gx), gx),
            "gy": lax.rem(iy + (dy % gy), gy),
        }

    own_rows = pl.ds(PAD, NX)
    own_planes = pl.ds(3, NZ)
    load_mask = pltpu.make_async_copy(mask_hbm, maskv, in_sem.at[0])
    load_rhs = pltpu.make_async_copy(rhs_hbm, edge.at[own_planes, 0, own_rows, :], in_sem.at[1])
    load_mask.start()
    load_rhs.start()

    partners = set((dz % gz, dx % gx, dy % gy) for dz, dx, dy in halo_offsets())
    partners |= set((0, 0, o) for o in range(1, gy))
    partners |= set((o, 0, 0) for o in range(1, gz))
    partners |= set((0, o, 0) for o in range(1, gx))
    partners = sorted(partners)
    barrier = pltpu.get_barrier_semaphore()
    for offset in partners:
        pl.semaphore_signal(barrier, inc=1, device_id=device(*offset), device_id_type=MESH)

    lane = lax.broadcasted_iota(jnp.int32, (NX, NY), 1)
    load_mask.wait()
    load_rhs.wait()
    edge[own_planes, 1, own_rows, :] = maskv[...].astype(F32).astype(BF16)
    packed = jnp.zeros((NX, NY), F32)
    for z in range(NZ):
        values = edge[3 + z, 0, own_rows, :].astype(F32)
        phases = maskv[z].astype(F32)
        packed = jnp.where(lane // 8 == z, pltpu.roll(values, 4 + 8 * z, 1), packed)
        packed = jnp.where(lane // 8 == z + 8, pltpu.roll(phases, 68 + 8 * z, 1), packed)
    pack[...] = packed.astype(BF16)
    pl.semaphore_wait(barrier, len(partners))

    z_from = {1: pl.ds(8, 3), -1: pl.ds(3, 3), 0: own_planes}
    z_to = {1: pl.ds(0, 3), -1: pl.ds(11, 3), 0: own_planes}
    z2_from = {1: pl.ds(9, 2), -1: pl.ds(3, 2), 0: own_planes}
    z2_to = {1: pl.ds(1, 2), -1: pl.ds(11, 2), 0: own_planes}
    x_from = {1: pl.ds(PAD + NX - 16, 16), -1: pl.ds(PAD, 16), 0: own_rows}
    x_to = {1: pl.ds(0, 16), -1: pl.ds(PAD + NX, 16), 0: own_rows}
    q_from = {1: pl.ds(NX - 16, 16), -1: pl.ds(0, 16), 0: pl.ds(0, NX)}
    copies = []
    for i, (dz, dx, dy) in enumerate(halo_offsets()):
        if dy == 0 and dx == 0:
            src = edge.at[z_from[dz], :, own_rows, :]
            dst = edge.at[z_to[dz], :, own_rows, :]
        elif dy == 0:
            src = edge.at[z2_from[dz], :, x_from[dx], :]
            dst = edge.at[z2_to[dz], :, x_to[dx], :]
        else:
            src = pack.at[q_from[dx], :]
            dst = (left if dy == 1 else right).at[1 - dz, x_to[dx], :]
        copy = pltpu.make_async_remote_copy(
            src_ref=src, dst_ref=dst, send_sem=hs.at[i], recv_sem=hr.at[i],
            device_id=device(dz, dx, dy), device_id_type=MESH,
        )
        copies.append(((dz == 0, abs(dz) + abs(dx) + abs(dy)), copy))
    for _, copy in sorted(copies, key=lambda c: c[0]):
        copy.start()
    for _, copy in copies:
        copy.wait_recv()

    half = lax.broadcasted_iota(jnp.int32, (HI - LO, NY), 1)
    low = lax.rem(half, 8) < 4
    first, last = half == 0, half == NY - 1

    def fill(side, base):
        joined = jnp.where(
            low, left[side].astype(F32)[LO:HI], right[side].astype(F32)[LO:HI]
        )

        def body(i, _):
            z, turn = base + i, i if side == 1 else (i + NZ - 3 if side == 0 else i)
            v0[z, 0, R, :] = edge[z, 0].astype(F32)[LO:HI]
            mk[z, 0, R, :] = edge[z, 1].astype(F32)[LO:HI]
            v0[z, 1, R, :] = pltpu.roll(joined, lax.rem(252 - 8 * turn, 128), 1)
            mk[z, 1, R, :] = pltpu.roll(joined, lax.rem(188 - 8 * turn, 128), 1)
            return 0

        lax.fori_loop(0, 3 if side != 1 else NZ, body, 0)

    fill(0, 0)
    fill(1, 3)
    fill(2, 11)

    def ahead(main, side):
        a, b = pltpu.roll(main, NY - 1, 1), pltpu.roll(side, NY - 1, 1)
        return jnp.where(last, b, a), jnp.where(last, a, b)

    def behind(main, side):
        a, b = pltpu.roll(main, 1, 1), pltpu.roll(side, 1, 1)
        return jnp.where(first, b, a), jnp.where(first, a, b)

    def weight(a, b):
        total = a + b
        return jnp.where(total < 0.5, GAS, jnp.where(total < 1.5, MIXED, LIQUID)).astype(F32)

    up, down = slice(LO + 1, HI + 1), slice(LO - 1, HI - 1)

    def fold(values):
        return jnp.sum(values.reshape(NX // 8, 8, NY), axis=0)

    def z_weights(z, _):
        for t in (0, 1):
            wz[z, t, R, :] = weight(mk[z, t, R, :], mk[z + 1, t, R, :])
        return 0

    lax.fori_loop(0, 13, z_weights, 0)

    def weights(z, _):
        here = [mk[z, t, R, :] for t in (0, 1)]
        there = ahead(*here)
        wy_now = [weight(a, b) for a, b in zip(here, there)]
        wy_back = behind(*wy_now)
        for t in (0, 1):
            wx_now = weight(here[t], mk[z, t, up, :])
            wx_back = weight(here[t], mk[z, t, down, :])
            total = mass_shift + wz[z, t, R, :] + wz[z - 1, t, R, :] + wx_now + wx_back
            total = total + wy_now[t] + wy_back[t]
            wx[z, t, R, :] = wx_now
            wy[z, t, R, :] = wy_now[t]
            di[z, t, R, :] = 1.0 / total
        return 0

    lax.fori_loop(1, 13, weights, 0)

    def image(field, z, sides):
        here = [field[z, t, R, :] for t in (0, 1)]
        there = ahead(*here)
        flow = [wy[z, t, R, :] * (here[t] - there[t]) for t in (0, 1)]
        back = behind(*flow)
        out = []
        for t in sides:
            v = here[t]
            total = mass_shift * v + wz[z, t, R, :] * (v - field[z + 1, t, R, :])
            total = total + wz[z - 1, t, R, :] * (v - field[z - 1, t, R, :])
            total = total + wx[z, t, R, :] * (v - field[z, t, up, :])
            total = total + wx[z, t, down, :] * (v - field[z, t, down, :])
            out.append(total + (flow[t] - back[t]))
        return here[0], out

    def advance(field, result, low_z, high_z, sides):
        def body(z, sums):
            here, totals = image(field, z, sides)
            for t, total in zip(sides, totals):
                now = total * di[z, t, R, :]
                result[z, t, R, :] = now
                if t == 0:
                    scale = jnp.where((z >= 3) & (z < 11), 1.0, 0.0).astype(F32)
                    owned = totals[0][OWN]
                    sums = (
                        sums[0] + scale * fold(here[OWN] * owned),
                        sums[1] + scale * fold(now[OWN] * owned),
                    )
            return sums

        zero = jnp.zeros((8, NY), F32)
        return lax.fori_loop(low_z, high_z, body, (zero, zero))

    def start_energy(z, total):
        v = v0[z, 0, pl.ds(PAD, NX), :]
        return total + fold(v * v / di[z, 0, pl.ds(PAD, NX), :])

    m0 = lax.fori_loop(3, 11, start_energy, jnp.zeros((8, NY), F32))
    m1, m2 = advance(v0, u1, 1, 13, (0, 1))
    m3, m4 = advance(u1, u2, 2, 12, (0, 1))
    m5, _ = advance(u2, u3, 3, 11, (0,))

    spot = lax.broadcasted_iota(jnp.int32, (1, NY), 1)
    row = jnp.zeros((1, NY), F32)
    for k, m in enumerate((m0, m1, m2, m3, m4, m5)):
        row = jnp.where(spot == k, jnp.sum(m, keepdims=True), row)

    place = 0
    for turn, (axis, n) in enumerate((("gy", gy), ("gz", gz), ("gx", gx))):
        mine[turn] = row
        sent = []
        for o in range(1, n):
            step = {"gz": 0, "gx": 0, "gy": 0}
            step[axis] = o
            copy = pltpu.make_async_remote_copy(
                src_ref=mine.at[turn], dst_ref=got.at[place],
                send_sem=rs.at[place], recv_sem=rr.at[place],
                device_id=device(step["gz"], step["gx"], step["gy"]), device_id_type=MESH,
            )
            copy.start()
            sent.append((place, copy))
            place += 1
        for at, copy in sent:
            copy.wait_recv()
            row = row + got[at]
        copies += [((), copy) for _, copy in sent]

    m = [jnp.sum(jnp.where(spot == k, row, 0.0), axis=1, keepdims=True) for k in range(6)]

    def inner(a, b):
        total = None
        for i, ai in enumerate(a):
            for j, bj in enumerate(b):
                if ai is None or bj is None:
                    continue
                term = ai * bj * m[i + j]
                total = term if total is None else total + term
        return total

    one = jnp.ones((1, 1), F32)
    z_poly, p_poly, x_poly, energy = [one], [one], [], m[0]
    for it in range(3):
        q_poly = [None] + p_poly
        step_size = energy / inner(p_poly, q_poly)
        x_poly = [
            step_size * p if i >= len(x_poly) else x_poly[i] + step_size * p
            for i, p in enumerate(p_poly)
        ]
        z_poly = [
            -step_size * q if i >= len(z_poly) else z_poly[i] if q is None else z_poly[i] - step_size * q
            for i, q in enumerate(q_poly)
        ]
        if it < 2:
            energy_next = inner(z_poly, z_poly)
            factor = energy_next / energy
            p_poly = [
                z_poly[i] if i >= len(p_poly) else z_poly[i] + factor * p_poly[i]
                for i in range(len(z_poly))
            ]
            energy = energy_next

    def finish(z, _):
        basis = [f[z + 3, 0, pl.ds(PAD, NX), :] for f in (v0, u1, u2, u3)]
        p_ref[z] = x_poly[0] * basis[0] + x_poly[1] * basis[1] + x_poly[2] * basis[2]
        r_ref[z] = (
            z_poly[0] * basis[0] + z_poly[1] * basis[1] + z_poly[2] * basis[2] + z_poly[3] * basis[3]
        )
        return 0

    lax.fori_loop(0, NZ, finish, 0)
    for _, copy in copies:
        copy.wait_send()


def solution(mesh):
    sizes = (mesh.shape["gz"], mesh.shape["gx"], mesh.shape["gy"])
    hops = sum(sizes) - 3
    field = pltpu.VMEM((14, 2, ROWS, NY), F32)

    def on_device(right_side, phase_mask):
        block = jax.ShapeDtypeStruct((NZ, NX, NY), F32)
        return pl.pallas_call(
            functools.partial(kernel, sizes),
            out_shape=(block, block),
            in_specs=[pl.BlockSpec(memory_space=pl.ANY)] * 2,
            out_specs=[pl.BlockSpec(memory_space=pltpu.VMEM)] * 2,
            scratch_shapes=[
                pltpu.VMEM((NZ, NX, NY), jnp.int32),
                pltpu.VMEM((14, 2, ROWS, NY), BF16),
                pltpu.VMEM((NX, NY), BF16),
                pltpu.VMEM((3, ROWS, NY), BF16),
                pltpu.VMEM((3, ROWS, NY), BF16),
                *([field] * 9),
                pltpu.VMEM((3, 1, NY), F32),
                pltpu.VMEM((hops, 1, NY), F32),
                pltpu.SemaphoreType.DMA((2,)),
                pltpu.SemaphoreType.DMA((26,)),
                pltpu.SemaphoreType.DMA((26,)),
                pltpu.SemaphoreType.DMA((hops,)),
                pltpu.SemaphoreType.DMA((hops,)),
            ],
            compiler_params=pltpu.CompilerParams(collective_id=0, has_side_effects=True),
        )(right_side, phase_mask)

    placed = P("gz", "gx", "gy")
    return jax.shard_map(
        on_device, mesh=mesh, in_specs=(placed, placed), out_specs=(placed, placed), check_vma=False
    )
```

time: 279 us -> 58.8 us (0.21)
  the two profiles are of different devices: /device:TPU:2 before, /device:TPU:1 now
where the time goes in v1:
time: 58.8 us; the launch traced here: 58.6 us
  Pallas kernels  55.5 us (94%)
  local copies, waits for them, and re-layouts  2.42 us (4%)
  between operations  0.65 us (1%)
    pallas_call x1, Pallas kernels, on_device(): pl.pallas_call(functools.partial(kernel, sizes), out_shape=(block, block)...  55.5 us
    unnamed x4, local copies, waits for them, and re-layouts  2.42 us

profile of v1, /device:TPU:1, one launch (start us, length us, event | category | flops | bytes accessed | tf_op | source)
XLA Modules:
  0.0 58.6 jit_solution(6375013781698390641)
XLA Ops:
  0.6 55.5 %shard_map.41 = (f32[8,64,128]{2,1,0:T(8,128)}, f32[8,64,128]{2,1,0:T(8,128)}) custom-call(bf16[8,64,128]{2,1,0:T(8,128)(2,1)} %rhs_hbm.1, s32[8,64,128]{2,1,0:T(8,128)} %mask_hbm.1), custom_call_target="tpu_custom_call" | custom-call | tf_op jit(solution)/shard_map/pallas_call | solution.py:291
  56.2 0.0 copy-start
  56.2 1.7 %copy.6 = f32[8,64,128]{2,1,0:T(8,128)} copy(f32[8,64,128]{2,1,0:T(8,128)} %get-tuple-element.4) | data formatting | bytes 524288
  57.9 0.0 copy-done
  57.9 0.7 %copy.7 = f32[8,64,128]{2,1,0:T(8,128)} copy(f32[8,64,128]{2,1,0:T(8,128)S(1)} %copy-done) | data formatting | bytes 524288
Async XLA Ops:
  56.2 1.7 %copy-start = (f32[8,64,128]{2,1,0:T(8,128)S(1)}, f32[8,64,128]{2,1,0:T(8,128)}, u32[]{:S(2)}) copy-start(f32[8,64,128]{2,1,0:T(8,128)} %get-tuple-element.5) | copy-start | bytes 786436

commit v2 on v1

v2 whole, which is shorter than its diff:
```python
import functools

import jax
import jax.numpy as jnp
from jax import lax
from jax.experimental import pallas as pl
from jax.experimental.pallas import tpu as pltpu
from jax.sharding import PartitionSpec as P

MESH = pl.DeviceIdType.MESH
F32 = jnp.float32
BF16 = jnp.bfloat16

mass_shift = 0.05
GAS = 1.0
MIXED = 2.0 / 1001.0
LIQUID = 0.001

NZ, NX, NY = 8, 64, 128
PAD = 16
ROWS = NX + 2 * PAD
LO, HI = PAD - 8, PAD + NX + 8
R = slice(LO, HI)
UP, DOWN = slice(LO + 1, HI + 1), slice(LO - 1, HI - 1)
OWN = slice(8, 8 + NX)


def halo_offsets():
    out = []
    for dz in (-1, 0, 1):
        for dx in (-1, 0, 1):
            for dy in (-1, 0, 1):
                if (dz, dx, dy) != (0, 0, 0):
                    out.append((dz, dx, dy))
    return out


def kernel(sizes, rhs_hbm, mask_hbm, b1, b2, b3, k0, k1, k2, k3, k4, k5, k6, maskv, edge, pack, left, right,
           v0, mk, wx, wy, wb, wz, di, u1, u2, u3, mine, got, in_sem, hs, hr, rs, rr, ready):
    gz, gx, gy = sizes
    iz, ix, iy = (lax.axis_index(a) for a in ("gz", "gx", "gy"))

    def device(dz, dx, dy):
        return {
            "gz": lax.rem(iz + (dz % gz), gz),
            "gx": lax.rem(ix + (dx % gx), gx),
            "gy": lax.rem(iy + (dy % gy), gy),
        }

    own_rows = pl.ds(PAD, NX)
    own_planes = pl.ds(3, NZ)
    load_mask = pltpu.make_async_copy(mask_hbm, maskv, in_sem.at[0])
    load_rhs = pltpu.make_async_copy(rhs_hbm, edge.at[own_planes, 0, own_rows, :], in_sem.at[1])
    load_mask.start()
    load_rhs.start()

    near = sorted(
        {(o % gz, 0, 0) for o in (1, -1)}
        | {(0, o % gx, 0) for o in (1, -1, 2, -2)}
        | {(0, 0, o % gy) for o in (1, -1)}
        - {(0, 0, 0)}
    )
    far = sorted(
        ({(o % gz, 0, 0) for o in (2, -2)}
        | {(0, o % gx, 0) for o in (4, -4)}
        | {(0, 0, o % gy) for o in (2, -2)})
        - {(0, 0, 0)}
    )

    def greet(semaphore, offsets):
        for offset in offsets:
            pl.semaphore_signal(semaphore, inc=1, device_id=device(*offset), device_id_type=MESH)

    barrier = pltpu.get_barrier_semaphore()
    greet(barrier, near)

    lane = lax.broadcasted_iota(jnp.int32, (NX, NY), 1)
    load_mask.wait()
    load_rhs.wait()
    edge[own_planes, 1, own_rows, :] = maskv[...].astype(F32).astype(BF16)
    packed = jnp.zeros((NX, NY), F32)
    for z in range(NZ):
        values = edge[3 + z, 0, own_rows, :].astype(F32)
        phases = maskv[z].astype(F32)
        packed = jnp.where(lane // 8 == z, pltpu.roll(values, 4 + 8 * z, 1), packed)
        packed = jnp.where(lane // 8 == z + 8, pltpu.roll(phases, 68 + 8 * z, 1), packed)
    pack[...] = packed.astype(BF16)
    pl.semaphore_wait(barrier, len(near))

    z_from = {1: pl.ds(8, 3), -1: pl.ds(3, 3), 0: own_planes}
    z_to = {1: pl.ds(0, 3), -1: pl.ds(11, 3), 0: own_planes}
    z2_from = {1: pl.ds(9, 2), -1: pl.ds(3, 2), 0: own_planes}
    z2_to = {1: pl.ds(1, 2), -1: pl.ds(11, 2), 0: own_planes}
    x_from = {1: pl.ds(PAD + NX - 16, 16), -1: pl.ds(PAD, 16), 0: own_rows}
    x_to = {1: pl.ds(0, 16), -1: pl.ds(PAD + NX, 16), 0: own_rows}
    q_from = {1: pl.ds(NX - 16, 16), -1: pl.ds(0, 16), 0: pl.ds(0, NX)}
    copies = []
    for dz, dx, dy in halo_offsets():
        if dy == 0 and dx == 0:
            src = edge.at[z_from[dz], :, own_rows, :]
            dst = edge.at[z_to[dz], :, own_rows, :]
        elif dy == 0:
            src = edge.at[z2_from[dz], :, x_from[dx], :]
            dst = edge.at[z2_to[dz], :, x_to[dx], :]
        else:
            src = pack.at[q_from[dx], :]
            dst = (left if dy == 1 else right).at[1 - dz, x_to[dx], :]
        copy = pltpu.make_async_remote_copy(
            src_ref=src, dst_ref=dst, send_sem=hs.at[0], recv_sem=hr.at[0 if dz == 0 else 1],
            device_id=device(dz, dx, dy), device_id_type=MESH,
        )
        copies.append((abs(dz) + abs(dx) + abs(dy), dz == 0, copy))
    for distance in (1, 2, 3):
        if distance > 1:
            greet(ready.at[distance - 2], near)
            pl.semaphore_wait(ready.at[distance - 2], len(near))
        for late in (False, True):
            for length, flat, copy in copies:
                if length == distance and flat == late:
                    copy.start()
    greet(ready.at[2], far)

    def settle(semaphore, ref):
        pltpu.make_async_copy(ref, ref, semaphore).wait()

    def arrived(early):
        settle(hr.at[0 if early else 1], v0.at[pl.ds(0, 11), 0, pl.ds(0, 32 if early else 64), :])

    half = lax.broadcasted_iota(jnp.int32, (1, NY), 1)
    low = lax.rem(half, 8) < 4
    first, last = half == 0, half == NY - 1

    def fill(side, base, count):
        joined = jnp.where(
            low, left[side].astype(F32)[LO:HI], right[side].astype(F32)[LO:HI]
        )

        def body(i, _):
            z = base + i
            turn = i + NZ - 3 if side == 0 else i
            v0[z, 0, R, :] = edge[z, 0].astype(F32)[LO:HI]
            mk[z, 0, R, :] = edge[z, 1].astype(F32)[LO:HI]
            v0[z, 1, R, :] = pltpu.roll(joined, lax.rem(252 - 8 * turn, 128), 1)
            mk[z, 1, R, :] = pltpu.roll(joined, lax.rem(188 - 8 * turn, 128), 1)
            return 0

        lax.fori_loop(0, count, body, 0, unroll=True)

    def ahead(main, side):
        a, b = pltpu.roll(main, NY - 1, 2), pltpu.roll(side, NY - 1, 2)
        return jnp.where(last, b, a), jnp.where(last, a, b)

    def behind(main, side):
        a, b = pltpu.roll(main, 1, 2), pltpu.roll(side, 1, 2)
        return jnp.where(first, b, a), jnp.where(first, a, b)

    def weight(a, b):
        total = a + b
        return jnp.where(total < 0.5, GAS, jnp.where(total < 1.5, MIXED, LIQUID)).astype(F32)

    def fold(values):
        return jnp.sum(values.reshape(NX // 8, 8, NY), axis=0)

    def weights(z, n, energy):
        here = [mk[pl.ds(z, n), t, R, :] for t in (0, 1)]
        after, before = ahead(*here), behind(*here)
        for t in (0, 1):
            across = weight(mk[pl.ds(z - 1, n + 1), t, R, :], mk[pl.ds(z, n + 1), t, R, :])
            wz[pl.ds(z - 1, n + 1), t, R, :] = across
            wx_now = weight(here[t], mk[pl.ds(z, n), t, UP, :])
            wx_back = weight(here[t], mk[pl.ds(z, n), t, DOWN, :])
            wy_now, wy_back = weight(here[t], after[t]), weight(here[t], before[t])
            total = mass_shift + across[1:] + across[:-1] + wx_now + wx_back + wy_now + wy_back
            wx[pl.ds(z, n), t, R, :] = wx_now
            wy[pl.ds(z, n), t, R, :] = wy_now
            wb[pl.ds(z, n), t, R, :] = wy_back
            di[pl.ds(z, n), t, R, :] = 1.0 / total
            if t == 0:
                v = v0[pl.ds(z, n), 0, R, :]
                for k in range(n):
                    scale = jnp.where((z + k >= 3) & (z + k < 11), 1.0, 0.0).astype(F32)
                    energy = energy + scale * fold((v[k] * v[k] * total[k])[OWN])
        return energy

    def image(field, z, n, sides, a, b):
        zs, rows = pl.ds(z, n), slice(a, b)
        here = [field[zs, t, rows, :] for t in (0, 1)]
        after, before = ahead(*here), behind(*here)
        out = []
        for t in sides:
            v = here[t]
            total = mass_shift * v
            total = total + wz[zs, t, rows, :] * (v - field[pl.ds(z + 1, n), t, rows, :])
            total = total + wz[pl.ds(z - 1, n), t, rows, :] * (v - field[pl.ds(z - 1, n), t, rows, :])
            total = total + wx[zs, t, rows, :] * (v - field[zs, t, a + 1 : b + 1, :])
            total = total + wx[zs, t, a - 1 : b - 1, :] * (v - field[zs, t, a - 1 : b - 1, :])
            total = total + wy[zs, t, rows, :] * (v - after[t])
            total = total + wb[zs, t, rows, :] * (v - before[t])
            out.append(total)
        return here[0], out

    def advance(field, result, groups, n, sums, ends=False):
        a, b = (PAD, PAD + NX) if ends else (LO, HI)
        inner_rows = slice(0, NX) if ends else OWN

        def body(i, sums):
            z = groups[0] + i * (groups[1] - groups[0]) if len(groups) > 1 else groups[0]
            here, totals = image(field, z, n, (0,) if ends else (0, 1), a, b)
            for t, total in enumerate(totals):
                now = total * di[pl.ds(z, n), t, a:b, :]
                result[pl.ds(z, n), t, a:b, :] = now
                if t == 0:
                    for k in range(n):
                        scale = jnp.where((z + k >= 3) & (z + k < 11), 1.0, 0.0).astype(F32)
                        owned = total[k][inner_rows]
                        sums = (
                            sums[0] + scale * fold(here[k][inner_rows] * owned),
                            sums[1] + scale * fold(now[k][inner_rows] * owned),
                        )
            return sums

        return lax.fori_loop(0, len(groups), body, sums)

    def lay(groups, n, energy):
        def body(i, energy):
            return weights(groups[0] + i * (groups[1] - groups[0]), n, energy)

        return lax.fori_loop(0, len(groups), body, energy)

    zero = jnp.zeros((8, NY), F32)
    s1 = s2 = s3 = (zero, zero)
    arrived(True)
    fill(1, 3, NZ)
    m0 = lay((4, 7), 3, zero)
    s1 = advance(v0, u1, (4, 7), 3, s1)
    s2 = advance(u1, u2, (5, 7), 2, s2)
    s3 = advance(u2, u3, (6,), 2, s3, True)
    arrived(False)
    fill(0, 0, 3)
    fill(2, 11, 3)
    m0 = lay((1, 10), 3, m0)
    s1 = advance(v0, u1, (1, 10), 3, s1)
    s2 = advance(u1, u2, (2, 9), 3, s2)
    s3 = advance(u2, u3, (3, 8), 3, s3, True)
    (m1, m2), (m3, m4), (m5, _) = s1, s2, s3

    spot = lax.broadcasted_iota(jnp.int32, (1, NY), 1)
    row = jnp.zeros((1, NY), F32)
    for k, m in enumerate((m0, m1, m2, m3, m4, m5)):
        row = jnp.where(spot == k, jnp.sum(m, keepdims=True), row)

    def keep(z, _):
        for out, field in ((b1, u1), (b2, u2), (b3, u3)):
            out[z] = field[z + 3, 0, pl.ds(PAD, NX), :]
        return 0

    pl.semaphore_wait(ready.at[2], len(far))
    place = 0
    for turn, (axis, n) in enumerate((("gy", gy), ("gz", gz), ("gx", gx))):
        mine[turn] = row
        for o in range(1, n):
            step = {"gz": 0, "gx": 0, "gy": 0}
            step[axis] = o
            pltpu.make_async_remote_copy(
                src_ref=mine.at[turn], dst_ref=got.at[place + o - 1],
                send_sem=rs.at[0], recv_sem=rr.at[turn],
                device_id=device(step["gz"], step["gx"], step["gy"]), device_id_type=MESH,
            ).start()
        if turn == 0:
            lax.fori_loop(0, NZ, keep, 0)
        settle(rr.at[turn], got.at[pl.ds(place, n - 1)])
        for o in range(1, n):
            row = row + got[place + o - 1]
        place += n - 1

    m = [jnp.sum(jnp.where(spot == k, row, 0.0), axis=1, keepdims=True) for k in range(6)]

    def inner(a, b):
        total = None
        for i, ai in enumerate(a):
            for j, bj in enumerate(b):
                if ai is None or bj is None:
                    continue
                term = ai * bj * m[i + j]
                total = term if total is None else total + term
        return total

    one = jnp.ones((1, 1), F32)
    z_poly, p_poly, x_poly, energy = [one], [one], [], m[0]
    for it in range(3):
        q_poly = [None] + p_poly
        step_size = energy / inner(p_poly, q_poly)
        x_poly = [
            step_size * p if i >= len(x_poly) else x_poly[i] + step_size * p
            for i, p in enumerate(p_poly)
        ]
        z_poly = [
            -step_size * q if i >= len(z_poly) else z_poly[i] if q is None else z_poly[i] - step_size * q
            for i, q in enumerate(q_poly)
        ]
        if it < 2:
            energy_next = inner(z_poly, z_poly)
            factor = energy_next / energy
            p_poly = [
                z_poly[i] if i >= len(p_poly) else z_poly[i] + factor * p_poly[i]
                for i in range(len(z_poly))
            ]
            energy = energy_next

    for out, c in zip((k0, k1, k2, k3, k4, k5, k6), x_poly + z_poly):
        out[...] = jnp.broadcast_to(c, (1, NY))
    settle(hs.at[0], v0.at[pl.ds(0, 11), 0])
    settle(rs.at[0], got)


def solution(mesh):
    sizes = (mesh.shape["gz"], mesh.shape["gx"], mesh.shape["gy"])
    hops = sum(sizes) - 3
    field = pltpu.VMEM((14, 2, ROWS, NY), F32)

    def on_device(right_side, phase_mask):
        block = jax.ShapeDtypeStruct((NZ, NX, NY), F32)
        coefficient = jax.ShapeDtypeStruct((1, NY), F32)
        u1, u2, u3, *coef = pl.pallas_call(
            functools.partial(kernel, sizes),
            out_shape=(block,) * 3 + (coefficient,) * 7,
            in_specs=[pl.BlockSpec(memory_space=pltpu.HBM)] * 2,
            out_specs=[pl.BlockSpec(memory_space=pltpu.VMEM)] * 10,
            scratch_shapes=[
                pltpu.VMEM((NZ, NX, NY), jnp.int32),
                pltpu.VMEM((14, 2, ROWS, NY), BF16),
                pltpu.VMEM((NX, NY), BF16),
                pltpu.VMEM((3, ROWS, NY), BF16),
                pltpu.VMEM((3, ROWS, NY), BF16),
                *([field] * 10),
                pltpu.VMEM((3, 1, NY), F32),
                pltpu.VMEM((hops, 1, NY), F32),
                pltpu.SemaphoreType.DMA((2,)),
                pltpu.SemaphoreType.DMA((1,)),
                pltpu.SemaphoreType.DMA((2,)),
                pltpu.SemaphoreType.DMA((1,)),
                pltpu.SemaphoreType.DMA((3,)),
                pltpu.SemaphoreType.REGULAR((3,)),
            ],
            compiler_params=pltpu.CompilerParams(
                collective_id=0, has_side_effects=True, vmem_limit_bytes=24 * 2**20
            ),
        )(*(pltpu.with_memory_space_constraint(a, pltpu.HBM) for a in (right_side, phase_mask)))
        u0 = right_side.astype(F32)
        c = [k[None] for k in coef]
        pressure = c[0] * u0 + c[1] * u1 + c[2] * u2
        return pressure, c[3] * u0 + c[4] * u1 + c[5] * u2 + c[6] * u3

    placed = P("gz", "gx", "gy")
    return jax.shard_map(
        on_device, mesh=mesh, in_specs=(placed, placed), out_specs=(placed, placed), check_vma=False
    )
```

time: 58.8 us -> 46.5 us (0.79)
  Pallas kernels: 55.5 us -> 44.8 us
  local copies, waits for them, and re-layouts: 2.42 us -> 0.01 us
  other arithmetic: 0 us -> 0.91 us
    pallas_call x1, Pallas kernels: 55.5 us -> 44.8 us  [on_device(): pl.pallas_call(functools.partial(kernel, sizes), out_shape=(block,) * 3 +...]
    unnamed x4 -> x2, local copies, waits for them, and re-layouts: 2.42 us -> 0.01 us
    add x0 -> x1, other arithmetic: none -> 0.91 us  [on_device(): return (pressure, c[3] * u0 + c[4] * u1 + c[5] * u2 + c[6] * u3)]
where the time goes in v2:
time: 46.5 us; the launch traced here: 46.3 us
  Pallas kernels  44.8 us (96%)
  other arithmetic  0.91 us (2%)
  between operations  0.65 us (1%)
    pallas_call x1, Pallas kernels, on_device(): pl.pallas_call(functools.partial(kernel, sizes), out_shape=(block,) * 3 +...  44.8 us

profile of v2, /device:TPU:1, one launch (start us, length us, event | category | flops | bytes accessed | tf_op | source)
XLA Modules:
  0.0 46.3 jit_solution(1419344968357289316)
XLA Ops:
  0.6 0.0 copy-start
  0.6 44.8 %shard_map.41 = (f32[8,64,128]{2,1,0:T(8,128)S(1)}, f32[8,64,128]{2,1,0:T(8,128)S(1)}, f32[8,64,128]{2,1,0:T(8,128)S(1)}, f32[1,128]{1,0:T(1,128)S(1)}, f32[1,12...) custom-call(bf16[8,64,128]{2,1,0:T(8,128)(2,1)} %rhs_hbm.1, ...), custom_call_target="tpu_custom_call" | custom-call | tf_op jit(solution)/shard_map/pallas_call | solution.py:324
  45.4 0.0 copy-done
  45.4 0.9 %fusion.4 = (f32[8,64,128]{2,1,0:T(8,128)}, f32[8,64,128]{2,1,0:T(8,128)}) fusion(bf16[8,64,128]{2,1,0:T(8,128)(2,1)S(1)} %copy-done, f32[8,64,128]{2,1,0:T(8,128)S(1)} %get-tuple-element.21, f32[8,64,128]{2,1,0:T(8,128)S(1)} %get-tuple-element.16, f32[8,64,128]{2,1,0:T(8,128)S(1)} %get-tuple-element.14, f32[128]{0:T(128)S(1)} %bitcast.13, ...), kind=kLoop, calls=%fused_computation.6 | loop fusion | flops 851968 | bytes 1445376 | tf_op jit(solution)/shard_map/add | solution.py:352
Async XLA Ops:
  0.6 44.8 %copy-start = (bf16[8,64,128]{2,1,0:T(8,128)(2,1)S(1)}, bf16[8,64,128]{2,1,0:T(8,128)(2,1)}, u32[]{:S(2)}) copy-start(bf16[8,64,128]{2,1,0:T(8,128)(2,1)} %rhs_hbm.1) | copy-start | bytes 393220

commit v3 on v2

v3 whole, which is shorter than its diff:
```python
import functools

import jax
import jax.numpy as jnp
from jax import lax
from jax.experimental import pallas as pl
from jax.experimental.pallas import tpu as pltpu
from jax.sharding import PartitionSpec as P

MESH = pl.DeviceIdType.MESH
F32 = jnp.float32
BF16 = jnp.bfloat16

mass_shift = 0.05
HALF_GAS, HALF_STEP = 0.5, 499.5

NZ, NX, NY = 8, 64, 128
PAD = 16
ROWS = NX + 2 * PAD
LO, HI = PAD - 8, PAD + NX + 8
R = slice(LO, HI)
UP, DOWN = slice(LO + 1, HI + 1), slice(LO - 1, HI - 1)
OWN = slice(8, 8 + NX)


def halo_offsets():
    out = []
    for dz in (-1, 0, 1):
        for dx in (-1, 0, 1):
            for dy in (-1, 0, 1):
                if (dz, dx, dy) != (0, 0, 0):
                    out.append((dz, dx, dy))
    return out


def two_sum(a, b):
    s = a + b
    t = s - a
    return s, (a - (s - t)) + (b - t)


def quick(a, b):
    s = a + b
    return s, b - (s - a)


def split(a):
    c = 4097.0 * a
    high = c - (c - a)
    return high, a - high


def times(a, b):
    p = a[0] * b[0]
    (ah, al), (bh, bl) = split(a[0]), split(b[0])
    error = ((ah * bh - p) + ah * bl + al * bh) + al * bl
    return quick(p, error + (a[0] * b[1] + a[1] * b[0]))


def minus(a, b, c):
    p, e = times(b, c)
    s, t = two_sum(a[0], -p)
    return quick(s, t + (a[1] - e))


def kernel(sizes, rhs_hbm, mask_hbm, b1, b2, b3, k0, k1, k2, k3, k4, k5, k6, maskv, edge, pack, left, right,
           v0, mk, wx, wy, wb, wz, di, u1, u2, u3, mine, got, in_sem, hs, hr, rs, rr, ready):
    gz, gx, gy = sizes
    iz, ix, iy = (lax.axis_index(a) for a in ("gz", "gx", "gy"))

    def device(dz, dx, dy):
        return {
            "gz": lax.rem(iz + (dz % gz), gz),
            "gx": lax.rem(ix + (dx % gx), gx),
            "gy": lax.rem(iy + (dy % gy), gy),
        }

    own_rows = pl.ds(PAD, NX)
    own_planes = pl.ds(3, NZ)
    load_mask = pltpu.make_async_copy(mask_hbm, maskv, in_sem.at[0])
    load_rhs = pltpu.make_async_copy(rhs_hbm, edge.at[own_planes, 0, own_rows, :], in_sem.at[1])
    load_mask.start()
    load_rhs.start()

    near = sorted(
        {(o % gz, 0, 0) for o in (1, -1)}
        | {(0, o % gx, 0) for o in (1, -1, 2, -2)}
        | {(0, 0, o % gy) for o in (1, -1)}
        - {(0, 0, 0)}
    )
    far = sorted(
        ({(o % gz, 0, 0) for o in (2, -2)}
        | {(0, o % gx, 0) for o in (4, -4)}
        | {(0, 0, o % gy) for o in (2, -2)})
        - {(0, 0, 0)}
    )

    distant = sorted(({(o % gz, 0, 0) for o in (4, -4)} | {(0, 0, o % gy) for o in (4, -4)}) - {(0, 0, 0)})

    wide = sorted(
        set(near)
        | {
            (dz % gz, dx % gx, dy % gy)
            for dz, dx, dy in halo_offsets()
            if abs(dz) + abs(dx) + abs(dy) <= 2
        }
    )

    def reach(offset):
        return sum(min(o, n - o) for o, n in zip(offset, sizes))

    def greet(semaphore, offsets):
        for offset in offsets:
            pl.semaphore_signal(semaphore, inc=1, device_id=device(*offset), device_id_type=MESH)

    barrier = pltpu.get_barrier_semaphore()
    greet(barrier, wide)

    lane = lax.broadcasted_iota(jnp.int32, (NX, NY), 1)
    load_mask.wait()
    load_rhs.wait()
    edge[own_planes, 1, own_rows, :] = maskv[...].astype(F32).astype(BF16)
    packed = jnp.zeros((NX, NY), F32)
    for z in range(NZ):
        values = edge[3 + z, 0, own_rows, :].astype(F32)
        phases = maskv[z].astype(F32)
        packed = jnp.where(lane // 8 == z, pltpu.roll(values, 4 + 8 * z, 1), packed)
        packed = jnp.where(lane // 8 == z + 8, pltpu.roll(phases, 68 + 8 * z, 1), packed)
    pack[...] = packed.astype(BF16)
    pl.semaphore_wait(barrier, len(wide))

    z_from = {1: pl.ds(8, 3), -1: pl.ds(3, 3), 0: own_planes}
    z_to = {1: pl.ds(0, 3), -1: pl.ds(11, 3), 0: own_planes}
    z2_from = {1: pl.ds(9, 2), -1: pl.ds(3, 2), 0: own_planes}
    z2_to = {1: pl.ds(1, 2), -1: pl.ds(11, 2), 0: own_planes}
    x_from = {1: pl.ds(PAD + NX - 16, 16), -1: pl.ds(PAD, 16), 0: own_rows}
    x_to = {1: pl.ds(0, 16), -1: pl.ds(PAD + NX, 16), 0: own_rows}
    q_from = {1: pl.ds(NX - 16, 16), -1: pl.ds(0, 16), 0: pl.ds(0, NX)}
    copies = []
    for dz, dx, dy in halo_offsets():
        if dy == 0 and dx == 0:
            src = edge.at[z_from[dz], :, own_rows, :]
            dst = edge.at[z_to[dz], :, own_rows, :]
        elif dy == 0:
            src = edge.at[z2_from[dz], :, x_from[dx], :]
            dst = edge.at[z2_to[dz], :, x_to[dx], :]
        else:
            src = pack.at[q_from[dx], :]
            dst = (left if dy == 1 else right).at[1 - dz, x_to[dx], :]
        copy = pltpu.make_async_remote_copy(
            src_ref=src, dst_ref=dst, send_sem=hs.at[0], recv_sem=hr.at[0 if dz == 0 else 1],
            device_id=device(dz, dx, dy), device_id_type=MESH,
        )
        copies.append((abs(dz) + abs(dx) + abs(dy), dz == 0, copy))
    for distance in (1, 2, 3):
        if distance == 3:
            greet(ready.at[0], near)
            pl.semaphore_wait(ready.at[0], len(near))
        for late in (False, True):
            for length, flat, copy in copies:
                if length == distance and flat == late:
                    copy.start()
    greet(ready.at[2], far)

    def settle(semaphore, ref):
        pltpu.make_async_copy(ref, ref, semaphore).wait()

    def arrived(late):
        settle(hr.at[late], v0.at[pl.ds(0, 11), 0, pl.ds(0, 64 if late else 32), :])

    half = lax.broadcasted_iota(jnp.int32, (1, NY), 1)
    low = lax.rem(half, 8) < 4
    first, last = half == 0, half == NY - 1

    def fill(side, base, count):
        joined = jnp.where(
            low, left[side].astype(F32)[LO:HI], right[side].astype(F32)[LO:HI]
        )

        halves = HALF_GAS + HALF_STEP * joined

        def body(i, _):
            z = base + i
            turn = i + NZ - 3 if side == 0 else i
            v0[z, 0, R, :] = edge[z, 0].astype(F32)[LO:HI]
            mk[z, 0, R, :] = HALF_GAS + HALF_STEP * edge[z, 1].astype(F32)[LO:HI]
            v0[z, 1, R, :] = pltpu.roll(joined, lax.rem(252 - 8 * turn, 128), 1)
            mk[z, 1, R, :] = pltpu.roll(halves, lax.rem(188 - 8 * turn, 128), 1)
            return 0

        lax.fori_loop(0, count, body, 0, unroll=True)

    def ahead(main, side):
        a, b = pltpu.roll(main, NY - 1, 2), pltpu.roll(side, NY - 1, 2)
        return jnp.where(last, b, a), jnp.where(last, a, b)

    def behind(main, side):
        a, b = pltpu.roll(main, 1, 2), pltpu.roll(side, 1, 2)
        return jnp.where(first, b, a), jnp.where(first, a, b)

    def weight(a, b):
        return 1.0 / (a + b)

    def owned(z, values):
        total = None
        for k in range(values.shape[0]):
            scale = jnp.where((z + k >= 3) & (z + k < 11), 1.0, 0.0).astype(F32)
            term = scale * values[k]
            total = term if total is None else total + term
        return total

    def weights(z, n, energy, only):
        zs = pl.ds(z, n)
        for a in range(PAD if only else LO, PAD + NX if only else HI, 8):
            rows = slice(a, a + 8)
            column = [mk[pl.ds(z - 1, n + 2), t, rows, :] for t in (0, 1)]
            here = [c[1:-1] for c in column]
            wy_now = [weight(p, q) for p, q in zip(here, ahead(*here))]
            wy_back = behind(*wy_now)
            for t in (0,) if only else (0, 1):
                across = weight(column[t][1:], column[t][:-1])
                wx_now = weight(here[t], mk[zs, t, a + 1 : a + 9, :])
                wx_back = weight(here[t], mk[zs, t, a - 1 : a + 7, :])
                total = mass_shift + across[1:] + across[:-1] + wx_now + wx_back
                total = total + wy_now[t] + wy_back[t]
                wz[pl.ds(z - 1, n + 1), t, rows, :] = across
                wx[zs, t, rows, :] = wx_now
                if only and a == PAD:
                    wx[zs, t, pl.ds(PAD - 8, 8), :] = weight(
                        mk[zs, t, pl.ds(PAD - 8, 8), :], mk[zs, t, pl.ds(PAD - 7, 8), :]
                    )
                wy[zs, t, rows, :] = wy_now[t]
                wb[zs, t, rows, :] = wy_back[t]
                di[zs, t, rows, :] = 1.0 / total
                if t == 0 and not only and PAD <= a < PAD + NX:
                    v = v0[zs, 0, rows, :]
                    energy = energy + owned(z, v * v * total)
        return energy

    def stencil(field, result, z, n, sums, only):
        zs = pl.ds(z, n)
        for a in range(PAD if only else LO, PAD + NX if only else HI, 8):
            rows, up, down = slice(a, a + 8), slice(a + 1, a + 9), slice(a - 1, a + 7)
            column = [field[pl.ds(z - 1, n + 2), t, rows, :] for t in (0, 1)]
            here = [c[1:-1] for c in column]
            after, before = ahead(*here), behind(*here)
            for t in (0,) if only else (0, 1):
                v, across = here[t], wz[pl.ds(z - 1, n + 1), t, rows, :]
                total = mass_shift * v + wy[zs, t, rows, :] * (v - after[t])
                total = total + wb[zs, t, rows, :] * (v - before[t])
                total = total + across[1:] * (v - column[t][2:])
                total = total + across[:-1] * (v - column[t][:-2])
                total = total + wx[zs, t, rows, :] * (v - field[zs, t, up, :])
                total = total + wx[zs, t, down, :] * (v - field[zs, t, down, :])
                now = total * di[zs, t, rows, :]
                result[zs, t, rows, :] = now
                if sums is not None and t == 0 and PAD <= a < PAD + NX:
                    sums = (sums[0] + owned(z, v * total), sums[1] + owned(z, now * total))
        return sums

    def at_turn(groups, i):
        return groups[0] + i * (groups[1] - groups[0]) if len(groups) > 1 else groups[0]

    def advance(field, result, groups, n, sums, ends=False, rims=None):
        def body(i, sums):
            if rims is not None:
                stencil(field, result, at_turn(rims, i), 1, None, True)
            return stencil(field, result, at_turn(groups, i), n, sums, ends)

        return lax.fori_loop(0, len(groups), body, sums)

    def lay(groups, n, energy, rims=None):
        def body(i, energy):
            if rims is not None:
                weights(at_turn(rims, i), 1, None, True)
            return weights(at_turn(groups, i), n, energy, False)

        return lax.fori_loop(0, len(groups), body, energy)

    zero = jnp.zeros((8, NY), F32)
    s1 = s2 = s3 = (zero, zero)
    arrived(0)
    fill(1, 3, NZ)
    m0 = lay((4, 7), 3, zero)
    s1 = advance(v0, u1, (4, 7), 3, s1)
    s2 = advance(u1, u2, (5, 7), 2, s2)
    s3 = advance(u2, u3, (6,), 2, s3, True)
    pl.semaphore_wait(ready.at[2], len(far))
    greet(ready.at[3], distant)
    arrived(1)
    fill(0, 0, 3)
    fill(2, 11, 3)
    m0 = lay((2, 10), 2, m0, (1, 12))
    s1 = advance(v0, u1, (2, 10), 2, s1, rims=(1, 12))
    s2 = advance(u1, u2, (3, 9), 2, s2, rims=(2, 11))
    s3 = advance(u2, u3, (3, 8), 3, s3, True)
    (m1, m2), (m3, m4), (m5, _) = s1, s2, s3

    spot = lax.broadcasted_iota(jnp.int32, (1, NY), 1)
    zero_row = jnp.zeros((1, NY), F32)
    row = jnp.zeros((1, NY), F32)
    for k, m in enumerate((m0, m1, m2, m3, m4, m5)):
        row = jnp.where(spot == k, jnp.sum(m, keepdims=True), row)

    def keep(z, _):
        for out, field in ((b1, u1), (b2, u2), (b3, u3)):
            out[z] = field[z + 3, 0, pl.ds(PAD, NX), :]
        return 0

    pl.semaphore_wait(ready.at[3], len(distant))
    place = 0
    plane = [(dz, 0, dy) for dz in range(gz) for dy in range(gy)]
    line = [(0, dx, 0) for dx in range(gx)]
    for turn, group in enumerate((plane, line)):
        group = sorted((o for o in group if o != (0, 0, 0)), key=lambda o: -reach(o))
        n = len(group)
        mine[turn] = row
        for i, offset in enumerate(group):
            pltpu.make_async_remote_copy(
                src_ref=mine.at[turn], dst_ref=got.at[place + i],
                send_sem=rs.at[0], recv_sem=rr.at[turn],
                device_id=device(*offset), device_id_type=MESH,
            ).start()
        if turn == 0:
            lax.fori_loop(0, NZ, keep, 0)
        settle(rr.at[turn], got.at[pl.ds(place, n)])
        pairs = [(row, zero_row)] + [(got[place + i], zero_row) for i in range(min(n, 7))]
        for i in range(7, n):
            high, rest = pairs[i % 8]
            high, error = two_sum(high, got[place + i])
            pairs[i % 8] = (high, rest + error)
        while len(pairs) > 1:
            joined_pairs = []
            for k in range(0, len(pairs) - 1, 2):
                high, error = two_sum(pairs[k][0], pairs[k + 1][0])
                joined_pairs.append((high, error + (pairs[k][1] + pairs[k + 1][1])))
            pairs = joined_pairs + pairs[len(pairs) // 2 * 2 :]
        high, rest = pairs[0]
        row = jnp.where(spot < NY // 2, high, high + pltpu.roll(rest, NY // 2, 1))
        place += n

    def at(k):
        return jnp.sum(jnp.where(spot == k, row, 0.0), axis=1, keepdims=True)

    m = [(at(k), at(k + NY // 2)) for k in range(6)]
    none = jnp.zeros((1, 1), F32)
    scale = (1.0 / m[0][0], none)
    m = [times(quick(*k), scale) for k in m]

    def cross(a, b, c, d):
        return minus(times(a, b), c, d)

    a11, a12 = cross(m[3], m[1], m[2], m[2]), cross(m[4], m[1], m[2], m[3])
    a22 = cross(m[5], m[1], m[3], m[3])
    c1, c2 = cross(m[1], m[1], m[2], m[0]), cross(m[2], m[1], m[3], m[0])
    x2 = cross(c2, a11, c1, a12)[0] / cross(a22, a11, a12, a12)[0]
    x1 = (c1[0] - a12[0] * x2) / a11[0]
    x0 = (m[0][0] - m[2][0] * x1 - m[3][0] * x2) / m[1][0]
    x_poly = [x0, x1, x2]
    z_poly = [jnp.ones((1, 1), F32)] + [-x for x in x_poly]
    for out, c in zip((k0, k1, k2, k3, k4, k5, k6), x_poly + z_poly):
        out[...] = jnp.broadcast_to(c, (1, NY))
    settle(hs.at[0], v0.at[pl.ds(0, 11), 0])
    settle(rs.at[0], got)


def solution(mesh):
    sizes = (mesh.shape["gz"], mesh.shape["gx"], mesh.shape["gy"])
    hops = sizes[0] * sizes[2] + sizes[1] - 2
    field = pltpu.VMEM((14, 2, ROWS, NY), F32)

    def on_device(right_side, phase_mask):
        block = jax.ShapeDtypeStruct((NZ, NX, NY), F32)
        coefficient = jax.ShapeDtypeStruct((1, NY), F32)
        u1, u2, u3, *coef = pl.pallas_call(
            functools.partial(kernel, sizes),
            out_shape=(block,) * 3 + (coefficient,) * 7,
            in_specs=[pl.BlockSpec(memory_space=pltpu.HBM)] * 2,
            out_specs=[pl.BlockSpec(memory_space=pltpu.VMEM)] * 10,
            scratch_shapes=[
                pltpu.VMEM((NZ, NX, NY), jnp.int32),
                pltpu.VMEM((14, 2, ROWS, NY), BF16),
                pltpu.VMEM((NX, NY), BF16),
                pltpu.VMEM((3, ROWS, NY), BF16),
                pltpu.VMEM((3, ROWS, NY), BF16),
                *([field] * 10),
                pltpu.VMEM((2, 1, NY), F32),
                pltpu.VMEM((hops, 1, NY), F32),
                pltpu.SemaphoreType.DMA((2,)),
                pltpu.SemaphoreType.DMA((1,)),
                pltpu.SemaphoreType.DMA((2,)),
                pltpu.SemaphoreType.DMA((1,)),
                pltpu.SemaphoreType.DMA((2,)),
                pltpu.SemaphoreType.REGULAR((4,)),
            ],
            compiler_params=pltpu.CompilerParams(
                collective_id=0, has_side_effects=True, vmem_limit_bytes=24 * 2**20
            ),
        )(*(pltpu.with_memory_space_constraint(a, pltpu.HBM) for a in (right_side, phase_mask)))
        u0 = right_side.astype(F32)
        c = [k[None] for k in coef]
        pressure = c[0] * u0 + c[1] * u1 + c[2] * u2
        return pressure, c[3] * u0 + c[4] * u1 + c[5] * u2 + c[6] * u3

    placed = P("gz", "gx", "gy")
    return jax.shard_map(
        on_device, mesh=mesh, in_specs=(placed, placed), out_specs=(placed, placed), check_vma=False
    )
```

time: 46.5 us -> 44 us (0.946)
  Pallas kernels: 44.8 us -> 42.3 us
    pallas_call x1, Pallas kernels: 44.8 us -> 42.3 us  [on_device(): pl.pallas_call(functools.partial(kernel, sizes), out_shape=(block,) * 3 +...]
where the time goes in v3:
time: 44 us; the launch traced here: 43.8 us
  Pallas kernels  42.3 us (96%)
  other arithmetic  0.91 us (2%)
  between operations  0.65 us (1%)
    pallas_call x1, Pallas kernels, on_device(): pl.pallas_call(functools.partial(kernel, sizes), out_shape=(block,) * 3 +...  42.3 us
    add x1, other arithmetic, on_device(): return (pressure, c[3] * u0 + c[4] * u1 + c[5] * u2 + c[6] * u3)  0.91 us

profile of v3, /device:TPU:1, one launch (start us, length us, event | category | flops | bytes accessed | tf_op | source)
XLA Modules:
  0.0 43.8 jit_solution(1744558230189514922)
XLA Ops:
  0.6 0.0 copy-start
  0.6 42.3 %shard_map.41 = (f32[8,64,128]{2,1,0:T(8,128)S(1)}, f32[8,64,128]{2,1,0:T(8,128)S(1)}, f32[8,64,128]{2,1,0:T(8,128)S(1)}, f32[1,128]{1,0:T(1,128)S(1)}, f32[1,12...) custom-call(bf16[8,64,128]{2,1,0:T(8,128)(2,1)} %rhs_hbm.1, ...), custom_call_target="tpu_custom_call" | custom-call | tf_op jit(solution)/shard_map/pallas_call | solution.py:375
  42.9 0.0 copy-done
  42.9 0.9 %fusion.4 = (f32[8,64,128]{2,1,0:T(8,128)}, f32[8,64,128]{2,1,0:T(8,128)}) fusion(bf16[8,64,128]{2,1,0:T(8,128)(2,1)S(1)} %copy-done, f32[8,64,128]{2,1,0:T(8,128)S(1)} %get-tuple-element.21, f32[8,64,128]{2,1,0:T(8,128)S(1)} %get-tuple-element.16, f32[8,64,128]{2,1,0:T(8,128)S(1)} %get-tuple-element.14, f32[128]{0:T(128)S(1)} %bitcast.13, ...), kind=kLoop, calls=%fused_computation.6 | loop fusion | flops 851968 | bytes 1445376 | tf_op jit(solution)/shard_map/add | solution.py:403
Async XLA Ops:
  0.6 42.3 %copy-start = (bf16[8,64,128]{2,1,0:T(8,128)(2,1)S(1)}, bf16[8,64,128]{2,1,0:T(8,128)(2,1)}, u32[]{:S(2)}) copy-start(bf16[8,64,128]{2,1,0:T(8,128)(2,1)} %rhs_hbm.1) | copy-start | bytes 393220

commit v4 on v3

--- a/solution.py
+++ b/solution.py
@@ -114,7 +114,7 @@
             pl.semaphore_signal(semaphore, inc=1, device_id=device(*offset), device_id_type=MESH)
 
     barrier = pltpu.get_barrier_semaphore()
-    greet(barrier, wide)
+    greet(barrier, sorted(wide, key=lambda o: -reach(o)))
 
     lane = lax.broadcasted_iota(jnp.int32, (NX, NY), 1)
     load_mask.wait()
@@ -198,6 +198,12 @@
         a, b = pltpu.roll(main, 1, 2), pltpu.roll(side, 1, 2)
         return jnp.where(first, b, a), jnp.where(first, a, b)
 
+    def beside(main, side):
+        return (
+            [pltpu.roll(jnp.where(first, side, main), NY - 1, 2)],
+            [pltpu.roll(jnp.where(last, side, main), 1, 2)],
+        )
+
     def weight(a, b):
         return 1.0 / (a + b)
 
@@ -215,8 +221,11 @@
             rows = slice(a, a + 8)
             column = [mk[pl.ds(z - 1, n + 2), t, rows, :] for t in (0, 1)]
             here = [c[1:-1] for c in column]
-            wy_now = [weight(p, q) for p, q in zip(here, ahead(*here))]
-            wy_back = behind(*wy_now)
+            if only:
+                wy_now, wy_back = ([weight(here[0], q[0])] for q in beside(*here))
+            else:
+                wy_now = [weight(p, q) for p, q in zip(here, ahead(*here))]
+                wy_back = behind(*wy_now)
             for t in (0,) if only else (0, 1):
                 across = weight(column[t][1:], column[t][:-1])
                 wx_now = weight(here[t], mk[zs, t, a + 1 : a + 9, :])
@@ -243,7 +252,7 @@
             rows, up, down = slice(a, a + 8), slice(a + 1, a + 9), slice(a - 1, a + 7)
             column = [field[pl.ds(z - 1, n + 2), t, rows, :] for t in (0, 1)]
             here = [c[1:-1] for c in column]
-            after, before = ahead(*here), behind(*here)
+            after, before = beside(*here) if only else (ahead(*here), behind(*here))
             for t in (0,) if only else (0, 1):
                 v, across = here[t], wz[pl.ds(z - 1, n + 1), t, rows, :]
                 total = mass_shift * v + wy[zs, t, rows, :] * (v - after[t])
@@ -280,13 +289,13 @@
     zero = jnp.zeros((8, NY), F32)
     s1 = s2 = s3 = (zero, zero)
     arrived(0)
+    pl.semaphore_wait(ready.at[2], len(far))
+    greet(ready.at[3], distant)
     fill(1, 3, NZ)
     m0 = lay((4, 7), 3, zero)
     s1 = advance(v0, u1, (4, 7), 3, s1)
     s2 = advance(u1, u2, (5, 7), 2, s2)
     s3 = advance(u2, u3, (6,), 2, s3, True)
-    pl.semaphore_wait(ready.at[2], len(far))
-    greet(ready.at[3], distant)
     arrived(1)
     fill(0, 0, 3)
     fill(2, 11, 3)
@@ -314,21 +323,28 @@
     for turn, group in enumerate((plane, line)):
         group = sorted((o for o in group if o != (0, 0, 0)), key=lambda o: -reach(o))
         n = len(group)
+        cut = n * 2 // 5 if turn == 0 else 0
         mine[turn] = row
         for i, offset in enumerate(group):
+            if turn == 0 and i == cut:
+                lax.fori_loop(0, NZ, keep, 0)
             pltpu.make_async_remote_copy(
                 src_ref=mine.at[turn], dst_ref=got.at[place + i],
-                send_sem=rs.at[0], recv_sem=rr.at[turn],
+                send_sem=rs.at[0], recv_sem=rr.at[2 * turn + (i < cut)],
                 device_id=device(*offset), device_id_type=MESH,
             ).start()
-        if turn == 0:
-            lax.fori_loop(0, NZ, keep, 0)
-        settle(rr.at[turn], got.at[pl.ds(place, n)])
-        pairs = [(row, zero_row)] + [(got[place + i], zero_row) for i in range(min(n, 7))]
-        for i in range(7, n):
-            high, rest = pairs[i % 8]
-            high, error = two_sum(high, got[place + i])
-            pairs[i % 8] = (high, rest + error)
+        pairs = [(row, zero_row)]
+        for kind, start, stop in ((0, cut, n), (1, 0, cut)):
+            if start == stop:
+                continue
+            settle(rr.at[2 * turn + kind], got.at[pl.ds(place + start, stop - start)])
+            for i in range(start, stop):
+                if len(pairs) < 8:
+                    pairs.append((got[place + i], zero_row))
+                    continue
+                high, rest = pairs[i % 8]
+                high, error = two_sum(high, got[place + i])
+                pairs[i % 8] = (high, rest + error)
         while len(pairs) > 1:
             joined_pairs = []
             for k in range(0, len(pairs) - 1, 2):
@@ -390,7 +406,7 @@
                 pltpu.SemaphoreType.DMA((1,)),
                 pltpu.SemaphoreType.DMA((2,)),
                 pltpu.SemaphoreType.DMA((1,)),
-                pltpu.SemaphoreType.DMA((2,)),
+                pltpu.SemaphoreType.DMA((3,)),
                 pltpu.SemaphoreType.REGULAR((4,)),
             ],
             compiler_params=pltpu.CompilerParams(

time: 44 us -> 43.7 us (level)
  no operation moved by 1% of the time
where the time goes in v4:
time: 43.7 us; the launch traced here: 43.6 us
  Pallas kernels  42 us (96%)
  other arithmetic  0.91 us (2%)
  between operations  0.65 us (1%)
    pallas_call x1, Pallas kernels, on_device(): pl.pallas_call(functools.partial(kernel, sizes), out_shape=(block,) * 3 +...  42 us
    add x1, other arithmetic, on_device(): return (pressure, c[3] * u0 + c[4] * u1 + c[5] * u2 + c[6] * u3)  0.91 us

profile of v4, /device:TPU:1, one launch (start us, length us, event | category | flops | bytes accessed | tf_op | source)
XLA Modules:
  0.0 43.6 jit_solution(8286231985506073188)
XLA Ops:
  0.6 0.0 copy-start
  0.6 42.0 %shard_map.41 = (f32[8,64,128]{2,1,0:T(8,128)S(1)}, f32[8,64,128]{2,1,0:T(8,128)S(1)}, f32[8,64,128]{2,1,0:T(8,128)S(1)}, f32[1,128]{1,0:T(1,128)S(1)}, f32[1,12...) custom-call(bf16[8,64,128]{2,1,0:T(8,128)(2,1)} %rhs_hbm.1, ...), custom_call_target="tpu_custom_call" | custom-call | tf_op jit(solution)/shard_map/pallas_call | solution.py:391
  42.7 0.0 copy-done
  42.7 0.9 %fusion.4 = (f32[8,64,128]{2,1,0:T(8,128)}, f32[8,64,128]{2,1,0:T(8,128)}) fusion(bf16[8,64,128]{2,1,0:T(8,128)(2,1)S(1)} %copy-done, f32[8,64,128]{2,1,0:T(8,128)S(1)} %get-tuple-element.21, f32[8,64,128]{2,1,0:T(8,128)S(1)} %get-tuple-element.16, f32[8,64,128]{2,1,0:T(8,128)S(1)} %get-tuple-element.14, f32[128]{0:T(128)S(1)} %bitcast.13, ...), kind=kLoop, calls=%fused_computation.6 | loop fusion | flops 851968 | bytes 1445376 | tf_op jit(solution)/shard_map/add | solution.py:419
Async XLA Ops:
  0.6 42.0 %copy-start = (bf16[8,64,128]{2,1,0:T(8,128)(2,1)S(1)}, bf16[8,64,128]{2,1,0:T(8,128)(2,1)}, u32[]{:S(2)}) copy-start(bf16[8,64,128]{2,1,0:T(8,128)(2,1)} %rhs_hbm.1) | copy-start | bytes 393220

commit v5 on v4

--- a/solution.py
+++ b/solution.py
@@ -316,28 +316,29 @@
             out[z] = field[z + 3, 0, pl.ds(PAD, NX), :]
         return 0
 
-    pl.semaphore_wait(ready.at[3], len(distant))
     place = 0
     plane = [(dz, 0, dy) for dz in range(gz) for dy in range(gy)]
     line = [(0, dx, 0) for dx in range(gx)]
-    for turn, group in enumerate((plane, line)):
+    for turn, group in enumerate((line, plane)):
         group = sorted((o for o in group if o != (0, 0, 0)), key=lambda o: -reach(o))
         n = len(group)
-        cut = n * 2 // 5 if turn == 0 else 0
+        cut = n * 2 // 5 if turn == 1 else 0
         mine[turn] = row
+        if turn == 1:
+            pl.semaphore_wait(ready.at[3], len(distant))
         for i, offset in enumerate(group):
-            if turn == 0 and i == cut:
-                lax.fori_loop(0, NZ, keep, 0)
             pltpu.make_async_remote_copy(
                 src_ref=mine.at[turn], dst_ref=got.at[place + i],
-                send_sem=rs.at[0], recv_sem=rr.at[2 * turn + (i < cut)],
+                send_sem=rs.at[0], recv_sem=rr.at[turn + (i < cut)],
                 device_id=device(*offset), device_id_type=MESH,
             ).start()
+        if turn == 0:
+            lax.fori_loop(0, NZ, keep, 0)
         pairs = [(row, zero_row)]
         for kind, start, stop in ((0, cut, n), (1, 0, cut)):
             if start == stop:
                 continue
-            settle(rr.at[2 * turn + kind], got.at[pl.ds(place + start, stop - start)])
+            settle(rr.at[turn + kind], got.at[pl.ds(place + start, stop - start)])
             for i in range(start, stop):
                 if len(pairs) < 8:
                     pairs.append((got[place + i], zero_row))

time: 43.7 us -> 43.6 us (level)
  no operation moved by 1% of the time
where the time goes in v5:
time: 43.6 us; the launch traced here: 43.5 us
  Pallas kernels  41.9 us (96%)
  other arithmetic  0.91 us (2%)
  between operations  0.65 us (1%)
    pallas_call x1, Pallas kernels, on_device(): pl.pallas_call(functools.partial(kernel, sizes), out_shape=(block,) * 3 +...  41.9 us
    add x1, other arithmetic, on_device(): return (pressure, c[3] * u0 + c[4] * u1 + c[5] * u2 + c[6] * u3)  0.91 us

profile of v5, /device:TPU:1, one launch (start us, length us, event | category | flops | bytes accessed | tf_op | source)
XLA Modules:
  0.0 43.5 jit_solution(8418779362623232263)
XLA Ops:
  0.6 0.0 copy-start
  0.6 41.9 %shard_map.41 = (f32[8,64,128]{2,1,0:T(8,128)S(1)}, f32[8,64,128]{2,1,0:T(8,128)S(1)}, f32[8,64,128]{2,1,0:T(8,128)S(1)}, f32[1,128]{1,0:T(1,128)S(1)}, f32[1,12...) custom-call(bf16[8,64,128]{2,1,0:T(8,128)(2,1)} %rhs_hbm.1, ...), custom_call_target="tpu_custom_call" | custom-call | tf_op jit(solution)/shard_map/pallas_call | solution.py:392
  42.6 0.0 copy-done
  42.6 0.9 %fusion.4 = (f32[8,64,128]{2,1,0:T(8,128)}, f32[8,64,128]{2,1,0:T(8,128)}) fusion(bf16[8,64,128]{2,1,0:T(8,128)(2,1)S(1)} %copy-done, f32[8,64,128]{2,1,0:T(8,128)S(1)} %get-tuple-element.21, f32[8,64,128]{2,1,0:T(8,128)S(1)} %get-tuple-element.16, f32[8,64,128]{2,1,0:T(8,128)S(1)} %get-tuple-element.14, f32[128]{0:T(128)S(1)} %bitcast.13, ...), kind=kLoop, calls=%fused_computation.6 | loop fusion | flops 851968 | bytes 1445376 | tf_op jit(solution)/shard_map/add | solution.py:420
Async XLA Ops:
  0.6 42.0 %copy-start = (bf16[8,64,128]{2,1,0:T(8,128)(2,1)S(1)}, bf16[8,64,128]{2,1,0:T(8,128)(2,1)}, u32[]{:S(2)}) copy-start(bf16[8,64,128]{2,1,0:T(8,128)(2,1)} %rhs_hbm.1) | copy-start | bytes 393220
